TPU v7x, 32 devices: a whole 2x2x4 slice. The times are simulated.
32 devices in a mesh: rows: 2 (over core), cols: 4 (over y, x), slabs: 4 (over z).
Axes of the slice: x: 2, y: 2, z: 4, core: 2. Of those that a mesh axis runs over, the one named last changes fastest.
Arguments:
- field_now: float32 [8, 128, 512, 128], P('rows', 'cols', 'slabs'), may hold values from 0.5 to 2
- earlier: float32 [8, 128, 512, 128], P('rows', 'cols', 'slabs'), may hold values from 0.2 to 1.8
- speed_square: float32 [8, 128, 512, 128], P('rows', 'cols', 'slabs'), may hold values from 0.05 to 0.3
Outputs:
- scaled_field: float32 [8, 128, 512, 128], P('rows', 'cols', 'slabs')
- field_now_end: float32 [8, 128, 512, 128], P('rows', 'cols', 'slabs')
All inputs are finite; a program needn't handle non-finite values.
Results may differ from a plain program's by a relative error of at most 0.00002.
Values sent between devices are 32-bit elements; how exact they have to be, the bound alone decides.
A program may use at most 128 MiB of HBM per device.

v0:
```python
import functools

import jax
import jax.numpy as jnp
from jax import lax
from jax.experimental import pallas as pl
from jax.experimental.pallas import tpu as pltpu
from jax.sharding import PartitionSpec as P

STEPS = 3
EPS = 1e-4
MESH = pl.DeviceIdType.MESH
AXES = ("rows", "cols", "slabs")


def march_kernel(
    counts, relay, now_hbm, old_hbm, speed_hbm, field, mean_ref, scale_ref,
    work, speed, face_out, face_in, own_stats, own_edge, in_stats, all_edge,
    relayed, load_x, load_y, load_c, send_sem, recv_sem, half_send, half_recv,
    pass_send, pass_recv, stat_send, stat_recv, edge_send, edge_recv,
):
    nj, ni, nk, lanes = now_hbm.shape
    n_slabs = counts["slabs"]
    parts = speed_parts(ni)
    width = ni // parts
    here = {axis: lax.axis_index(axis) for axis in AXES}
    has_low = {axis: here[axis] > 0 for axis in AXES}
    has_high = {axis: here[axis] < counts[axis] - 1 for axis in AXES}

    inner = (pl.ds(1, nj), pl.ds(1, ni))
    copy_x = pltpu.make_async_copy(now_hbm, work.at[inner], load_x)
    copy_x.start()
    copies = []
    for part in range(parts):
        span, padded = pl.ds(part * width, width), pl.ds(1 + part * width, width)
        copies.append((
            pltpu.make_async_copy(old_hbm.at[:, span], field.at[pl.ds(1, nj), padded], load_y.at[part]),
            pltpu.make_async_copy(speed_hbm.at[:, span], speed.at[:, span], load_c.at[part]),
        ))
        for copy in copies[-1]:
            copy.start()

    barrier = pltpu.get_barrier_semaphore()
    expected = jnp.int32(n_slabs - 1)
    for axis in ("rows", "cols"):
        for there, shift in ((has_low[axis], -1), (has_high[axis], 1)):
            expected = expected + there.astype(jnp.int32)

            @pl.when(there)
            def _():
                pl.semaphore_signal(barrier, inc=1, device_id={axis: here[axis] + shift}, device_id_type=MESH)

    peers = [lax.rem(here["slabs"] + gap, n_slabs) for gap in range(1, n_slabs)]
    for peer in peers:
        pl.semaphore_signal(barrier, inc=1, device_id={"slabs": peer}, device_id_type=MESH)
    if relay:
        over = lax.rem(here["cols"] + 2, 4)
        pl.semaphore_signal(barrier, inc=1, device_id={"cols": over}, device_id_type=MESH)
        expected = expected + 1
    pl.semaphore_wait(barrier, expected)

    half = nj // 2 if relay else 0

    def half_copy(step, to_high, kind):
        buffer = work if step % 2 == 0 else field
        edge = ni - 1 if to_high else 0
        source = now_hbm.at[pl.ds(0, half), edge] if step == 0 else buffer.at[pl.ds(1, half), edge + 1]
        landing = buffer.at[pl.ds(1, half), 0 if to_high else ni + 1]
        sems = half_send.at[step, int(to_high)], half_recv.at[step, int(to_high)]
        target = here["cols"] + (1 if to_high else -1)
        if kind == "to":
            landing, target = relayed.at[step], over
            sems = sems[0], pass_recv.at[step]
        elif kind == "on":
            source, target = relayed.at[step], here["cols"] + (-1 if to_high else 1)
            sems = pass_send.at[step], sems[1]
        return pltpu.make_async_remote_copy(
            source, landing, *sems, device_id={"cols": target}, device_id_type=MESH
        )

    def halves(step, what):
        if not relay:
            return
        me = here["cols"]
        for to_high, source, target in ((True, 1, 2), (False, 2, 1)):
            edge_sends = (me == 0) | (me == 2) if to_high else (me == 1) | (me == 3)
            if what == "start":
                pl.when(me == source)(half_copy(step, to_high, "to").start)
                pl.when(edge_sends)(half_copy(step, to_high, "straight").start)
            elif what == "pass":
                @pl.when(me == (3 if to_high else 0))
                def _():
                    half_copy(step, to_high, "to").wait_recv()
                    half_copy(step, to_high, "on").start()
            elif what == "sent":
                pl.when(has_high["cols"] if to_high else has_low["cols"])(
                    half_copy(step, to_high, "straight").wait_send
                )
                pl.when(me == (3 if to_high else 0))(half_copy(step, to_high, "on").wait_send)
            else:
                pl.when(has_low["cols"] if to_high else has_high["cols"])(
                    half_copy(step, to_high, "straight").wait_recv
                )

    def face_copy(step, axis, to_high):
        buffer = work if step % 2 == 0 else field
        number = 2 * AXES.index(axis) + int(to_high)
        target = here[axis] + (1 if to_high else -1)
        if axis == "slabs":
            source, landing = face_out.at[step, int(to_high)], face_in.at[step, int(to_high)]
        elif axis == "cols":
            edge = ni - 1 if to_high else 0
            rest = pl.ds(half, nj - half)
            source = now_hbm.at[rest, edge] if step == 0 else buffer.at[pl.ds(1 + half, nj - half), edge + 1]
            landing = buffer.at[pl.ds(1 + half, nj - half), 0 if to_high else ni + 1]
        else:
            edge = nj - 1 if to_high else 0
            source = now_hbm.at[edge] if step == 0 else buffer.at[edge + 1, pl.ds(1, ni)]
            landing = buffer.at[0 if to_high else nj + 1, pl.ds(1, ni)]
        return pltpu.make_async_remote_copy(
            source, landing, send_sem.at[step, number], recv_sem.at[step, number],
            device_id={axis: target}, device_id_type=MESH,
        )

    def exchange(step, axis, what):
        if axis == "cols":
            halves(step, what)
        for to_high in (False, True):
            sends = has_high[axis] if to_high else has_low[axis]
            takes = has_low[axis] if to_high else has_high[axis]
            copy = face_copy(step, axis, to_high)
            if what == "start":
                pl.when(sends)(copy.start)
            elif what == "sent":
                pl.when(sends)(copy.wait_send)
            else:
                pl.when(takes)(copy.wait_recv)

    exchange(0, "cols", "start")
    exchange(0, "rows", "start")

    zeros_line = jnp.zeros((nk, lanes), jnp.float32)
    for buffer in (work, field):
        for absent, edge in ((~has_low["rows"], 0), (~has_high["rows"], nj + 1)):
            @pl.when(absent)
            def _():
                @pl.loop(1, ni + 1)
                def _(i):
                    buffer[edge, i] = zeros_line
        for absent, edge in ((~has_low["cols"], 0), (~has_high["cols"], ni + 1)):
            @pl.when(absent)
            def _():
                @pl.loop(1, nj + 1)
                def _(j):
                    buffer[j, edge] = zeros_line
    for absent, side in ((~has_low["slabs"], 1), (~has_high["slabs"], 0)):
        @pl.when(absent)
        def _():
            for step in range(STEPS):
                face_in[step, side] = jnp.zeros((nj, ni, lanes), jnp.float32)
    own_stats[...] = jnp.zeros_like(own_stats)

    copy_x.wait()

    @pl.loop(0, ni)
    def _(i):
        for j in range(nj):
            face_out[0, 0, j, pl.ds(i, 1), :] = work[j + 1, i + 1, pl.ds(0, 1), :]
            face_out[0, 1, j, pl.ds(i, 1), :] = work[j + 1, i + 1, pl.ds(nk - 1, 1), :]

    exchange(0, "slabs", "start")

    groups = nk // 8
    row_number = lax.broadcasted_iota(jnp.int32, (8, lanes), 0)

    def line(step, i, edge_side=None):
        now, old = (work, field) if step % 2 == 1 else (field, work)
        last = step == STEPS
        sums = [None] * nj
        for g in range(groups):
            k = pl.ds(8 * g, 8)
            column = [now[j, i, k, :] for j in range(nj + 2)]
            for j in range(1, nj + 1):
                middle = column[j]
                if g == 0:
                    low = jnp.where(
                        row_number == 0,
                        jnp.broadcast_to(face_in[step - 1, 1, j - 1, pl.ds(i - 1, 1), :], (8, lanes)),
                        pltpu.roll(middle, 1, 0),
                    )
                else:
                    low = now[j, i, pl.ds(8 * g - 1, 8), :]
                if g == groups - 1:
                    high = jnp.where(
                        row_number == 7,
                        jnp.broadcast_to(face_in[step - 1, 0, j - 1, pl.ds(i - 1, 1), :], (8, lanes)),
                        pltpu.roll(middle, 7, 0),
                    )
                else:
                    high = now[j, i, pl.ds(8 * g + 1, 8), :]
                spread = (
                    (column[j - 1] + column[j + 1])
                    + (now[j, i - 1, k, :] + now[j, i + 1, k, :])
                    + (low + high)
                    - 6.0 * middle
                )
                later = 2.0 * middle - old[j, i, k, :] + speed[j - 1, i - 1, k, :] * spread
                old[j, i, k, :] = later
                if last:
                    sums[j - 1] = later if g == 0 else sums[j - 1] + later
                else:
                    if g == 0:
                        face_out[step, 0, j - 1, pl.ds(i - 1, 1), :] = later[0:1]
                    if g == groups - 1:
                        face_out[step, 1, j - 1, pl.ds(i - 1, 1), :] = later[7:8]
        if last:
            for j in range(nj):
                total = jnp.sum(sums[j], axis=0, keepdims=True)
                mean = jnp.broadcast_to(total * (1.0 / nk), (8, lanes))
                squares = None
                for g in range(groups):
                    moved = old[j + 1, i, pl.ds(8 * g, 8), :] - mean
                    squares = moved * moved if g == 0 else squares + moved * moved
                square = jnp.sum(squares, axis=0, keepdims=True)
                if edge_side is None:
                    own_stats[0, 0, j, pl.ds(i - 1, 1), :] = total
                    own_stats[0, 1, j, pl.ds(i - 1, 1), :] = square
                else:
                    own_edge[0, pl.ds(edge_side * nj + j, 1), :] = total
                    own_edge[1, pl.ds(edge_side * nj + j, 1), :] = square

    def lines(step, start, stop):
        @pl.loop(start, stop)
        def _(i):
            line(step, i)

    levels = n_slabs.bit_length() - 1
    partners = []
    for level in range(levels):
        bit = lax.rem(here["slabs"] // 2**level, 2)
        partners.append(here["slabs"] + (1 - 2 * bit) * 2**level)

    def stat_copy(part, level):
        rows = pl.ds(part * width, width)
        return pltpu.make_async_remote_copy(
            own_stats.at[level, :, :, rows], in_stats.at[level, :, :, rows],
            stat_send.at[part, level], stat_recv.at[part, level],
            device_id={"slabs": partners[level]}, device_id_type=MESH,
        )

    def edge_copy(gap):
        return pltpu.make_async_remote_copy(
            own_edge, all_edge.at[gap - 1], edge_send.at[gap - 1], edge_recv.at[gap - 1],
            device_id={"slabs": peers[gap - 1]}, device_id_type=MESH,
        )

    def merged(part, level):
        rows = pl.ds(part * width, width)
        stat_copy(part, level).wait_recv()
        mine, theirs = own_stats[level, :, :, rows, :], in_stats[level, :, :, rows, :]
        cells = float(nk * 2**level)
        apart = (theirs[0] - mine[0]) * (1.0 / cells)
        return mine[0] + theirs[0], mine[1] + theirs[1] + (0.5 * cells) * apart * apart

    def advance(part, level):
        rows = pl.ds(part * width, width)
        total, square = merged(part, level)
        own_stats[level + 1, 0, :, rows, :] = total
        own_stats[level + 1, 1, :, rows, :] = square
        stat_copy(part, level + 1).start()

    gaps = range(1, n_slabs)
    for step in range(1, STEPS + 1):
        if step == 3:
            for axis in AXES:
                exchange(1, axis, "sent")
        exchange(step - 1, "rows", "taken")
        exchange(step - 1, "slabs", "taken")
        for part in range(parts):
            if step == 1:
                for copy in copies[part]:
                    copy.wait()
            start, stop = 1 + part * width, 1 + (part + 1) * width
            lines(step, max(start, 2), min(stop, ni))
            if part == 0:
                halves(step - 1, "pass")
            if step == STEPS:
                stat_copy(part, 0).start()
                if part >= 2 and levels > 1:
                    advance(part - 2, 0)
        if step == STEPS and levels > 1:
            for part in range(max(parts - 2, 0), parts):
                advance(part, 0)
        exchange(step - 1, "cols", "taken")
        line(step, 1, 0)
        line(step, ni, 1)
        if step < STEPS:
            for axis in ("cols", "slabs", "rows"):
                exchange(step, axis, "start")
    for gap in gaps:
        edge_copy(gap).start()
    for level in range(1, levels - 1):
        for part in range(parts):
            advance(part, level)

    whole = float(nk * n_slabs)

    def combine(own, others):
        mean = own[0]
        for other in others:
            mean = mean + other[0]
        mean = mean * (1.0 / whole)
        square = None
        for one in (own, *others):
            gap = one[0] * (1.0 / nk) - mean
            term = one[1] + nk * gap * gap
            square = term if square is None else square + term
        return mean, lax.rsqrt(square * (1.0 / whole) + EPS)

    for part in range(parts):
        rows = pl.ds(part * width, width)
        total, square = merged(part, levels - 1)
        mean_ref[:, rows, :] = total * (1.0 / whole)
        scale_ref[:, rows, :] = lax.rsqrt(square * (1.0 / whole) + EPS)
    for gap in gaps:
        edge_copy(gap).wait_recv()
    mean, scale = combine(own_edge[...], [all_edge[gap - 1] for gap in gaps])
    for side, i in ((0, 0), (1, ni - 1)):
        for j in range(nj):
            place = side * nj + j
            mean_ref[j, pl.ds(i, 1), :] = mean[place:place + 1]
            scale_ref[j, pl.ds(i, 1), :] = scale[place:place + 1]

    for step in range(STEPS):
        if step != 1:
            for axis in AXES:
                exchange(step, axis, "sent")
    for part in range(parts):
        for level in range(levels):
            stat_copy(part, level).wait_send()
    for gap in gaps:
        edge_copy(gap).wait_send()


def speed_parts(ni):
    return 4 if ni % 32 == 0 else 1


def scale_kernel(field, mean_ref, scale_ref, scaled_hbm, field_hbm, scaled, out_sem, field_sem):
    nj, ni, nk, lanes = scaled_hbm.shape
    parts = speed_parts(ni)
    width = ni // parts
    field_copies = [
        pltpu.make_async_copy(field.at[j + 1, pl.ds(1, ni)], field_hbm.at[j], field_sem.at[j])
        for j in range(nj)
    ]
    out_copies = []
    for j in range(nj):
        for part in range(parts):
            @pl.loop(part * width, (part + 1) * width)
            def _(i):
                mean = jnp.broadcast_to(mean_ref[j, pl.ds(i, 1), :], (8, lanes))
                scale = jnp.broadcast_to(scale_ref[j, pl.ds(i, 1), :], (8, lanes))
                for g in range(nk // 8):
                    k = pl.ds(8 * g, 8)
                    scaled[j, i, k, :] = (field[j + 1, i + 1, k, :] - mean) * scale

            rows = pl.ds(part * width, width)
            copy = pltpu.make_async_copy(
                scaled.at[j, rows], scaled_hbm.at[j, rows], out_sem.at[j, part]
            )
            copy.start()
            out_copies.append(copy)
            if part == 0:
                field_copies[j].start()
    for copy in (*field_copies, *out_copies):
        copy.wait()


def shards(counts, relay, field_now, earlier, speed_square):
    nj, ni, nk, lanes = field_now.shape
    n_slabs = counts["slabs"]
    levels = n_slabs.bit_length() - 1
    assert n_slabs == 2**levels and levels >= 1
    relay = relay and nj > 1
    parts = speed_parts(ni)
    f32 = jnp.float32
    padded = (nj + 2, ni + 2, nk, lanes)
    hbm = pl.BlockSpec(memory_space=pltpu.HBM)
    vmem = pl.BlockSpec(memory_space=pltpu.VMEM)
    cells = nj * ni * nk * lanes
    dma = pltpu.SemaphoreType.DMA
    field, mean, scale = pl.pallas_call(
        functools.partial(march_kernel, counts, relay),
        name="march",
        out_shape=(
            pltpu.VMEM(padded, f32),
            pltpu.VMEM((nj, ni, lanes), f32),
            pltpu.VMEM((nj, ni, lanes), f32),
        ),
        in_specs=[hbm] * 3,
        out_specs=(vmem,) * 3,
        scratch_shapes=[
            pltpu.VMEM(padded, f32),
            pltpu.VMEM((nj, ni, nk, lanes), f32),
            pltpu.VMEM((STEPS, 2, nj, ni, lanes), f32),
            pltpu.VMEM((STEPS, 2, nj, ni, lanes), f32),
            pltpu.VMEM((levels, 2, nj, ni, lanes), f32),
            pltpu.VMEM((2, 2 * nj, lanes), f32),
            pltpu.VMEM((levels, 2, nj, ni, lanes), f32),
            pltpu.VMEM((n_slabs - 1, 2, 2 * nj, lanes), f32),
            pltpu.VMEM((STEPS, max(nj // 2, 1), nk, lanes), f32),
            dma(()),
            dma((parts,)),
            dma((parts,)),
            dma((STEPS, 6)),
            dma((STEPS, 6)),
            dma((STEPS, 2)),
            dma((STEPS, 2)),
            dma((STEPS,)),
            dma((STEPS,)),
            dma((parts, levels)),
            dma((parts, levels)),
            dma((n_slabs - 1,)),
            dma((n_slabs - 1,)),
        ],
        compiler_params=pltpu.CompilerParams(
            collective_id=0, has_side_effects=True, vmem_limit_bytes=45 * 2**20
        ),
        cost_estimate=pl.CostEstimate(flops=33 * cells, bytes_accessed=12 * cells, transcendentals=0),
    )(field_now, earlier, speed_square)
    return pl.pallas_call(
        scale_kernel,
        name="scale",
        out_shape=(jax.ShapeDtypeStruct(field_now.shape, f32),) * 2,
        in_specs=[vmem] * 3,
        out_specs=(hbm,) * 2,
        scratch_shapes=[
            pltpu.VMEM((nj, ni, nk, lanes), f32),
            dma((nj, parts)),
            dma((nj,)),
        ],
        compiler_params=pltpu.CompilerParams(vmem_limit_bytes=16 * 2**20),
        cost_estimate=pl.CostEstimate(flops=2 * cells, bytes_accessed=8 * cells, transcendentals=0),
    )(field, mean, scale)


def crosses(mesh):
    order = ("rows", "cols", "slabs")
    devices = mesh.devices.transpose([mesh.axis_names.index(axis) for axis in order])
    if devices.shape[1] != 4:
        return False
    one, other = (getattr(devices[0, place, 0], "coords", None) for place in (1, 2))
    return one is not None and sum(a != b for a, b in zip(one, other)) > 1


def solution(mesh):
    spec = P("rows", "cols", "slabs", None)
    return jax.shard_map(
        functools.partial(shards, dict(mesh.shape), crosses(mesh)),
        mesh=mesh,
        in_specs=(spec,) * 3,
        out_specs=(spec,) * 2,
        check_vma=False,
    )
```

profile of v0, /device:TPU:0, one launch (start us, length us, event | category | flops | bytes accessed | tf_op | source)
XLA Modules:
  0.0 51.7 jit_solution(8737286688752405201)
XLA Ops:
  0.6 45.0 %march.1 = (f32[6,34,128,128]{3,2,1,0:T(8,128)S(1)}, f32[4,32,128]{2,1,0:T(8,128)S(1)}, f32[4,32,128]{2,1,0:T(8,128)S(1)}) custom-call(f32[4,32,128,128]{3,2,1,0:T(8,128)} %now_hbm.1, f32[4,32,128,128]{3,2,1,0:T(8,128)} %old_hbm.1, f32[4,32,128,128]{3,2,1,0:T(8,128)} %speed_hbm.1), custom_call_target="tpu_custom_call" | custom-call | flops 69206016 | bytes 25165824 | tf_op jit(solution)/shard_map/march/pallas_call | solution.py:393
  45.6 6.0 %scale.1 = (f32[4,32,128,128]{3,2,1,0:T(8,128)}, f32[4,32,128,128]{3,2,1,0:T(8,128)}) custom-call(f32[6,34,128,128]{3,2,1,0:T(8,128)S(1)} %get-tuple-element.5.field, f32[4,32,128]{2,1,0:T(8,128)S(1)} %get-tuple-element.6.mean_ref, f32[4,32,128]{2,1,0:T(8,128)S(1)} %get-tuple-element.7.scale_ref), custom_call_target="tpu_custom_call" | custom-call | flops 4194304 | bytes 16777216 | tf_op jit(solution)/shard_map/scale/pallas_call | solution.py:432
where the time goes:
time: 51.8 us; the launch traced here: 51.7 us
  Pallas kernels  51 us (98%)
  between operations  0.64 us (1%)
    pallas_call x1, Pallas kernels, shards(): pl.pallas_call(functools.partial(march_kernel, counts, relay), name='marc...  45 us
    pallas_call x1, Pallas kernels, shards(): pl.pallas_call(scale_kernel, name='scale', out_shape=(jax.ShapeDtypeStruc...  6.04 us

commit v1 on v0

v1 whole, which is shorter than its diff:
```python
import functools

import jax
import jax.numpy as jnp
from jax import lax
from jax.experimental import pallas as pl
from jax.experimental.pallas import tpu as pltpu
from jax.sharding import PartitionSpec as P

STEPS = 3
EPS = 1e-4
MESH = pl.DeviceIdType.MESH
AXES = ("rows", "cols", "slabs")
OWN, DIAG = 0, 1


def line_parts(ni):
    return 4 if ni % 32 == 0 else 1


def edge_places(cols, ni):
    odd = lax.rem(cols, 2)
    return ni - odd * (ni - 1), 1 + odd * (ni - 1)


def march_kernel(
    counts, relay, now_hbm, old_hbm, speed_hbm, field, scaled, mean_ref, scale_ref,
    work, face_out, face_in, rim_out, rim_in, own_stats, own_edge, in_stats, all_edge, relayed,
    means, scales, load_x, load_y, load_c,
    side_send, side_recv, pass_send, pass_recv, row_send, row_recv, row_rim_send, row_rim_recv,
    slab_send, slab_recv, slab_rim_send, slab_rim_recv, stat_send, stat_recv, edge_send, edge_recv,
):
    nj, ni, nk, lanes = now_hbm.shape
    speed = scaled
    n_slabs = counts["slabs"]
    parts = line_parts(ni)
    width = ni // parts
    inside_out = [0, *range(parts - 1, 0, -1)] if parts > 1 else [0]
    outside_in = inside_out[2:] + inside_out[:2]
    here = {axis: lax.axis_index(axis) for axis in AXES}
    has_low = {axis: here[axis] > 0 for axis in AXES}
    has_high = {axis: here[axis] < counts[axis] - 1 for axis in AXES}
    odd = lax.rem(here["cols"], 2)
    places = edge_places(here["cols"], ni)
    beside = (here["cols"] + 1 - 2 * odd, here["cols"] - 1 + 2 * odd)
    has_side = tuple((other >= 0) & (other < counts["cols"]) for other in beside)
    halos = ((1 - odd) * (ni + 1), odd * (ni + 1))

    def span(part):
        return part * width, (part + 1) * width

    loads = {}
    for name, source in (("now", now_hbm), ("old", old_hbm), ("speed", speed_hbm)):
        for part in inside_out:
            start, _ = span(part)
            plain, padded = pl.ds(start, width), (pl.ds(1, nj), pl.ds(1 + start, width))
            target = {"now": work.at[padded], "old": field.at[padded], "speed": speed.at[:, plain]}[name]
            sem = {"now": load_x, "old": load_y, "speed": load_c}[name].at[part]
            loads[name, part] = pltpu.make_async_copy(source.at[:, plain], target, sem)
            loads[name, part].start()

    barrier = pltpu.get_barrier_semaphore()
    expected = jnp.int32(n_slabs - 1)
    for axis in ("rows", "cols"):
        for there, shift in ((has_low[axis], -1), (has_high[axis], 1)):
            expected = expected + there.astype(jnp.int32)

            @pl.when(there)
            def _():
                pl.semaphore_signal(barrier, inc=1, device_id={axis: here[axis] + shift}, device_id_type=MESH)

    peers = [lax.rem(here["slabs"] + gap, n_slabs) for gap in range(1, n_slabs)]
    for peer in peers:
        pl.semaphore_signal(barrier, inc=1, device_id={"slabs": peer}, device_id_type=MESH)
    if relay:
        over = lax.rem(here["cols"] + 2, 4)
        pl.semaphore_signal(barrier, inc=1, device_id={"cols": over}, device_id_type=MESH)
        expected = expected + 1
    pl.semaphore_wait(barrier, expected)

    half = nj // 2 if relay else 0
    relays = has_side[OWN] & ~has_side[DIAG]

    def buffer_of(step):
        return work if step % 2 == 0 else field

    def side_copy(step, which, j, kind="straight"):
        buffer = buffer_of(step)
        source = now_hbm.at[j, places[which] - 1] if step == 0 else buffer.at[j + 1, places[which]]
        target = beside[which]
        landing = buffer.at[j + 1, ni + 1 - halos[which]]
        sems = side_send.at[step, which, j], side_recv.at[step, which, j]
        if kind == "to":
            landing, target = relayed.at[step, j], over
            sems = sems[0], pass_recv.at[step, j]
        elif kind == "on":
            source, target = relayed.at[step, j], beside[OWN]
            landing = buffer.at[j + 1, halos[OWN]]
            sems = pass_send.at[step, j], sems[1]
        return pltpu.make_async_remote_copy(
            source, landing, *sems, device_id={"cols": target}, device_id_type=MESH
        )

    def side(step, which, j, what):
        relayed_line = which == DIAG and j < half
        if what == "start":
            pl.when(has_side[which])(side_copy(step, which, j, "to" if relayed_line else "straight").start)
        elif what == "sent":
            pl.when(has_side[which])(side_copy(step, which, j).wait_send)
        else:
            pl.when(has_side[which])(side_copy(step, which, j).wait_recv)

    def hand_on(step, j):
        if j < half:
            @pl.when(relays)
            def _():
                side_copy(step, DIAG, j, "to").wait_recv()
                side_copy(step, DIAG, j, "on").start()

    def run(copy, sends, takes, what):
        if what == "start":
            pl.when(sends)(copy.start)
        elif what == "sent":
            pl.when(sends)(copy.wait_send)
        else:
            pl.when(takes)(copy.wait_recv)

    def directions(axis):
        for to_high in (0, 1):
            sends = has_high[axis] if to_high else has_low[axis]
            takes = has_low[axis] if to_high else has_high[axis]
            yield to_high, sends, takes, here[axis] + (1 if to_high else -1)

    def segment(step, number):
        if number < parts:
            start, stop = span(number)
            rim = 1 if step < 2 else 2
            return max(1 + start, 1 + rim), min(1 + stop, 1 + ni - rim)
        place = 2 if number == parts else ni - 1
        return place, place + 1

    def rows(step, number, what):
        start, stop = segment(step, number)
        lines, buffer = pl.ds(start, stop - start), buffer_of(step)
        for to_high, sends, takes, target in directions("rows"):
            j = nj - 1 if to_high else 0
            source = now_hbm.at[j, pl.ds(start - 1, stop - start)] if step == 0 else buffer.at[j + 1, lines]
            copy = pltpu.make_async_remote_copy(
                source, buffer.at[0 if to_high else nj + 1, lines],
                row_send.at[step, to_high, number], row_recv.at[step, to_high, number],
                device_id={"rows": target}, device_id_type=MESH,
            )
            run(copy, sends, takes, what)

    def row_rim(step, which, to_highs, what):
        buffer = buffer_of(step)
        for to_high, sends, takes, target in directions("rows"):
            if to_high not in to_highs:
                continue
            j = nj - 1 if to_high else 0
            source = now_hbm.at[j, places[which] - 1] if step == 0 else buffer.at[j + 1, places[which]]
            copy = pltpu.make_async_remote_copy(
                source, buffer.at[0 if to_high else nj + 1, places[which]],
                row_rim_send.at[step, to_high, which], row_rim_recv.at[step, to_high, which],
                device_id={"rows": target}, device_id_type=MESH,
            )
            run(copy, sends, takes, what)

    def slabs(step, number, what):
        start, stop = segment(step, number)
        lines = pl.ds(start - 1, stop - start)
        for to_high, sends, takes, target in directions("slabs"):
            copy = pltpu.make_async_remote_copy(
                face_out.at[step, to_high, lines], face_in.at[step, to_high, lines],
                slab_send.at[step, to_high, number], slab_recv.at[step, to_high, number],
                device_id={"slabs": target}, device_id_type=MESH,
            )
            run(copy, sends, takes, what)

    def slab_rim(step, which, what):
        for to_high, sends, takes, target in directions("slabs"):
            copy = pltpu.make_async_remote_copy(
                rim_out.at[step, to_high, which], rim_in.at[step, to_high, which],
                slab_rim_send.at[step, to_high, which], slab_rim_recv.at[step, to_high, which],
                device_id={"slabs": target}, device_id_type=MESH,
            )
            run(copy, sends, takes, what)

    for j in range(half):
        side(0, DIAG, j, "start")
    for j in range(nj):
        side(0, OWN, j, "start")
    for j in range(half, nj):
        side(0, DIAG, j, "start")
    for which in (OWN, DIAG):
        row_rim(0, which, (0, 1), "start")
    for part in inside_out:
        rows(0, part, "start")

    zeros_line = jnp.zeros((nk, lanes), jnp.float32)
    for buffer in (work, field):
        for absent, edge in ((~has_low["rows"], 0), (~has_high["rows"], nj + 1)):
            @pl.when(absent)
            def _():
                @pl.loop(1, ni + 1)
                def _(i):
                    buffer[edge, i] = zeros_line
        for absent, edge in ((~has_low["cols"], 0), (~has_high["cols"], ni + 1)):
            @pl.when(absent)
            def _():
                @pl.loop(1, nj + 1)
                def _(j):
                    buffer[j, edge] = zeros_line
    for absent, to_high in ((~has_low["slabs"], 1), (~has_high["slabs"], 0)):
        @pl.when(absent)
        def _():
            for step in range(STEPS):
                face_in[step, to_high] = jnp.zeros((ni, nj, lanes), jnp.float32)
                rim_in[step, to_high] = jnp.zeros((2, nj, lanes), jnp.float32)
    own_stats[...] = jnp.zeros_like(own_stats)

    for part in inside_out:
        loads["now", part].wait()
        if part == inside_out[min(1, parts - 1)]:
            for which in (OWN, DIAG):
                for j in range(nj):
                    rim_out[0, 0, which, pl.ds(j, 1), :] = work[j + 1, places[which], pl.ds(0, 1), :]
                    rim_out[0, 1, which, pl.ds(j, 1), :] = work[j + 1, places[which], pl.ds(nk - 1, 1), :]
            for which in (OWN, DIAG):
                slab_rim(0, which, "start")
        start, stop = segment(0, part)

        @pl.loop(start, stop)
        def _(i):
            for j in range(nj):
                face_out[0, 0, i - 1, pl.ds(j, 1), :] = work[j + 1, i, pl.ds(0, 1), :]
                face_out[0, 1, i - 1, pl.ds(j, 1), :] = work[j + 1, i, pl.ds(nk - 1, 1), :]

        slabs(0, part, "start")

    groups = nk // 8
    row_number = lax.broadcasted_iota(jnp.int32, (8, lanes), 0)

    def line(step, i, js, rim=None):
        now, old = (work, field) if step % 2 == 1 else (field, work)
        last = step == STEPS
        sums = {}

        def halo(to_high, j):
            if rim is None:
                return face_in[step - 1, to_high, i - 1, pl.ds(j, 1), :]
            return rim_in[step - 1, to_high, rim, pl.ds(j, 1), :]

        def keep(to_high, j, row):
            if rim is None:
                face_out[step, to_high, i - 1, pl.ds(j, 1), :] = row
            else:
                rim_out[step, to_high, rim, pl.ds(j, 1), :] = row

        for g in range(groups):
            k = pl.ds(8 * g, 8)
            column = {j: now[j, i, k, :] for j in range(js[0], js[-1] + 3)}
            for j in js:
                middle = column[j + 1]
                if g == 0:
                    low = jnp.where(
                        row_number == 0, jnp.broadcast_to(halo(1, j), (8, lanes)), pltpu.roll(middle, 1, 0)
                    )
                else:
                    low = now[j + 1, i, pl.ds(8 * g - 1, 8), :]
                if g == groups - 1:
                    high = jnp.where(
                        row_number == 7, jnp.broadcast_to(halo(0, j), (8, lanes)), pltpu.roll(middle, 7, 0)
                    )
                else:
                    high = now[j + 1, i, pl.ds(8 * g + 1, 8), :]
                spread = (
                    (column[j] + column[j + 2])
                    + (now[j + 1, i - 1, k, :] + now[j + 1, i + 1, k, :])
                    + (low + high)
                    - 6.0 * middle
                )
                later = 2.0 * middle - old[j + 1, i, k, :] + speed[j, i - 1, k, :] * spread
                old[j + 1, i, k, :] = later
                if last:
                    sums[j] = later if g == 0 else sums[j] + later
                else:
                    if g == 0:
                        keep(0, j, later[0:1])
                    if g == groups - 1:
                        keep(1, j, later[7:8])
        if last:
            for j in js:
                total = jnp.sum(sums[j], axis=0, keepdims=True)
                mean = jnp.broadcast_to(total * (1.0 / nk), (8, lanes))
                squares = None
                for g in range(groups):
                    moved = old[j + 1, i, pl.ds(8 * g, 8), :] - mean
                    squares = moved * moved if g == 0 else squares + moved * moved
                square = jnp.sum(squares, axis=0, keepdims=True)
                if rim is None:
                    own_stats[0, 0, j, pl.ds(i - 1, 1), :] = total
                    own_stats[0, 1, j, pl.ds(i - 1, 1), :] = square
                else:
                    own_edge[0, pl.ds(rim * nj + j, 1), :] = total
                    own_edge[1, pl.ds(rim * nj + j, 1), :] = square

    every_j = tuple(range(nj))

    def interior(step, part):
        start, stop = span(part)
        rim = max(step, 1)
        start, stop = max(1 + start, 1 + rim), min(1 + stop, 1 + ni - rim)
        if step == 1:
            loads["old", part].wait()
            loads["speed", part].wait()
        rows(step - 1, part, "taken")
        slabs(step - 1, part, "taken")
        if step == 3:
            rows(1, part, "sent")

        @pl.loop(start, stop)
        def _(i):
            line(step, i, every_j)

        if step < STEPS:
            rows(step, part, "start")
            slabs(step, part, "start")

    def strips(step):
        if step == 2:
            for number, place in ((parts, 2), (parts + 1, ni - 1)):
                line(step, place, every_j)
                rows(step, number, "start")
                slabs(step, number, "start")
        else:
            for number in (parts, parts + 1):
                rows(step - 1, number, "taken")
                slabs(step - 1, number, "taken")
            for place in (3, ni - 2, 2, ni - 1):
                line(step, place, every_j)

    def edge(step, which, j):
        side(step - 1, which, j, "taken")
        order = edge_order[which]
        if j == order[0]:
            slab_rim(step - 1, which, "taken")
            if step == 3:
                row_rim(1, which, (0, 1), "sent")
        if j == 0:
            row_rim(step - 1, which, (1,), "taken")
        if j == nj - 1:
            row_rim(step - 1, which, (0,), "taken")
        if step == 3:
            side(1, which, j, "sent")
        line(step, places[which], (j,), which)
        if step < STEPS:
            side(step, which, j, "start")
            if j == 0:
                row_rim(step, which, (0,), "start")
            if j == nj - 1:
                row_rim(step, which, (1,), "start")
            if j == order[-1]:
                slab_rim(step, which, "start")

    edge_order = (
        list(range(nj)),
        [j for pair in zip(range(half), range(half, nj)) for j in pair] + list(range(2 * half, nj))
        if half else list(range(nj)),
    )

    levels = n_slabs.bit_length() - 1
    partners = []
    for level in range(levels):
        bit = lax.rem(here["slabs"] // 2**level, 2)
        partners.append(here["slabs"] + (1 - 2 * bit) * 2**level)

    def stat_copy(part, level):
        lines = pl.ds(part * width, width)
        return pltpu.make_async_remote_copy(
            own_stats.at[level, :, :, lines], in_stats.at[level, :, :, lines],
            stat_send.at[part, level], stat_recv.at[part, level],
            device_id={"slabs": partners[level]}, device_id_type=MESH,
        )

    def edge_copy(gap):
        return pltpu.make_async_remote_copy(
            own_edge, all_edge.at[gap - 1], edge_send.at[gap - 1], edge_recv.at[gap - 1],
            device_id={"slabs": peers[gap - 1]}, device_id_type=MESH,
        )

    def merged(part, level):
        lines = pl.ds(part * width, width)
        stat_copy(part, level).wait_recv()
        mine, theirs = own_stats[level, :, :, lines, :], in_stats[level, :, :, lines, :]
        cells = float(nk * 2**level)
        apart = (theirs[0] - mine[0]) * (1.0 / cells)
        return mine[0] + theirs[0], mine[1] + theirs[1] + (0.5 * cells) * apart * apart

    def advance(part, level):
        lines = pl.ds(part * width, width)
        total, square = merged(part, level)
        own_stats[level + 1, 0, :, lines, :] = total
        own_stats[level + 1, 1, :, lines, :] = square
        stat_copy(part, level + 1).start()

    whole = float(nk * n_slabs)

    def rescale(part):
        lines = pl.ds(part * width, width)
        total, square = merged(part, levels - 1)
        means[:, lines, :] = total * (1.0 / whole)
        scales[:, lines, :] = lax.rsqrt(square * (1.0 / whole) + EPS)
        start, stop = span(part)

        @pl.loop(max(start, 1), min(stop, ni - 1))
        def _(i):
            for j in range(nj):
                mean = jnp.broadcast_to(means[j, pl.ds(i, 1), :], (8, lanes))
                scale = jnp.broadcast_to(scales[j, pl.ds(i, 1), :], (8, lanes))
                for g in range(groups):
                    k = pl.ds(8 * g, 8)
                    scaled[j, i, k, :] = (field[j + 1, i + 1, k, :] - mean) * scale

    def do(kind, *what):
        if kind == "in":
            interior(what[0], what[1])
        elif kind == "own":
            edge(what[0], OWN, edge_order[OWN][what[1]])
        elif kind == "diag":
            edge(what[0], DIAG, edge_order[DIAG][what[1]])
        elif kind == "pass":
            hand_on(*what)
        elif kind == "strips":
            strips(what[0])
        elif kind == "stats":
            stat_copy(what[0], 0).start()
        elif kind == "advance":
            for level in range(levels - 1):
                advance(what[0], level)
        elif kind == "rescale":
            rescale(what[0])

    for what in agenda(nj, parts, inside_out, outside_in):
        do(*what)

    gaps = range(1, n_slabs)
    for gap in gaps:
        edge_copy(gap).start()
    for part in outside_in:
        rescale(part)

    def combine(own, others):
        mean = own[0]
        for other in others:
            mean = mean + other[0]
        mean = mean * (1.0 / whole)
        square = None
        for one in (own, *others):
            gap = one[0] * (1.0 / nk) - mean
            term = one[1] + nk * gap * gap
            square = term if square is None else square + term
        return mean, lax.rsqrt(square * (1.0 / whole) + EPS)

    for step in range(STEPS):
        for which in (OWN, DIAG):
            for j in range(nj):
                if step != 1:
                    side(step, which, j, "sent")
            if step != 1:
                row_rim(step, which, (0, 1), "sent")
            slab_rim(step, which, "sent")
        for j in range(half):
            pl.when(relays)(side_copy(step, DIAG, j, "on").wait_send)
        for number in range(parts + 2 if step == 2 else parts):
            if step != 1:
                rows(step, number, "sent")
            slabs(step, number, "sent")
    for part in range(parts):
        for level in range(levels):
            stat_copy(part, level).wait_send()
    for gap in gaps:
        edge_copy(gap).wait_recv()
    mean, scale = combine(own_edge[...], [all_edge[gap - 1] for gap in gaps])
    mean_ref[...] = mean
    scale_ref[...] = scale
    for gap in gaps:
        edge_copy(gap).wait_send()


def agenda(nj, parts, first, last):
    passes = [[("pass", step, j) for j in range(nj)] for step in range(STEPS)]
    own = {step: [("own", step, n) for n in range(nj)] for step in range(1, STEPS + 1)}
    diag = {step: [("diag", step, n) for n in range(nj)] for step in range(1, STEPS + 1)}
    fill = {step: [("in", step, part) for part in (last if step == 3 else first)] for step in (1, 2, 3)}
    order = []

    def put(*lists):
        for some in lists:
            order.extend(some)

    def weave(*lists):
        spots = [((n + 0.5) / len(some), number, entry) for number, some in enumerate(lists) for n, entry in enumerate(some)]
        order.extend(entry for _, _, entry in sorted(spots, key=lambda spot: spot[:2]))

    two = max(parts // 2, 1)
    half = nj // 2
    put(fill[1][:1])
    weave(fill[1][1:], [entry for n in range(nj) for entry in (passes[0][n], own[1][n])])
    weave(diag[1], fill[2][:two])
    put([("strips", 2)])
    weave([entry for n in range(nj) for entry in (passes[1][n], own[2][n])], fill[2][two:] + fill[3][:1])
    weave(diag[2], fill[3][1:two + 1])
    put(fill[3][two + 1:])
    put([("strips", 3)])
    stats = [("stats", part) for part in last]
    put(stats)
    weave([entry for n in range(nj) for entry in (passes[2][n], own[3][n])], [("advance", part) for part in last])
    put(diag[3])
    return order


def finish_kernel(field, scaled, mean_ref, scale_ref, scaled_hbm, field_hbm, rims, field_sem, scaled_sem, rim_sem):
    nj, ni, nk, lanes = scaled_hbm.shape
    copies = []
    for j in range(nj):
        copies.append(pltpu.make_async_copy(field.at[j + 1, pl.ds(1, ni)], field_hbm.at[j], field_sem.at[j]))
        inner = pl.ds(1, ni - 2)
        copies.append(pltpu.make_async_copy(scaled.at[j, inner], scaled_hbm.at[j, inner], scaled_sem.at[j]))
    for copy in copies:
        copy.start()
    places = edge_places(lax.axis_index("cols"), ni)
    for which in (OWN, DIAG):
        for j in range(nj):
            row = pl.ds(which * nj + j, 1)
            mean = jnp.broadcast_to(mean_ref[row, :], (8, lanes))
            scale = jnp.broadcast_to(scale_ref[row, :], (8, lanes))
            for g in range(nk // 8):
                k = pl.ds(8 * g, 8)
                rims[which, j, k, :] = (field[j + 1, places[which], k, :] - mean) * scale
        copy = pltpu.make_async_copy(rims.at[which], scaled_hbm.at[:, places[which] - 1], rim_sem.at[which])
        copy.start()
        copies.append(copy)
    for copy in copies:
        copy.wait()


def shards(counts, relay, field_now, earlier, speed_square):
    nj, ni, nk, lanes = field_now.shape
    n_slabs = counts["slabs"]
    levels = n_slabs.bit_length() - 1
    assert n_slabs == 2**levels and levels >= 1
    relay = relay and nj > 1
    parts = line_parts(ni)
    f32 = jnp.float32
    padded = (nj + 2, ni + 2, nk, lanes)
    hbm = pl.BlockSpec(memory_space=pltpu.HBM)
    vmem = pl.BlockSpec(memory_space=pltpu.VMEM)
    cells = nj * ni * nk * lanes
    dma = pltpu.SemaphoreType.DMA
    field, scaled, mean, scale = pl.pallas_call(
        functools.partial(march_kernel, counts, relay),
        name="march",
        out_shape=(
            pltpu.VMEM(padded, f32),
            pltpu.VMEM((nj, ni, nk, lanes), f32),
            pltpu.VMEM((2 * nj, lanes), f32),
            pltpu.VMEM((2 * nj, lanes), f32),
        ),
        in_specs=[hbm] * 3,
        out_specs=(vmem,) * 4,
        scratch_shapes=[
            pltpu.VMEM(padded, f32),
            pltpu.VMEM((STEPS, 2, ni, nj, lanes), f32),
            pltpu.VMEM((STEPS, 2, ni, nj, lanes), f32),
            pltpu.VMEM((STEPS, 2, 2, nj, lanes), f32),
            pltpu.VMEM((STEPS, 2, 2, nj, lanes), f32),
            pltpu.VMEM((levels, 2, nj, ni, lanes), f32),
            pltpu.VMEM((2, 2 * nj, lanes), f32),
            pltpu.VMEM((levels, 2, nj, ni, lanes), f32),
            pltpu.VMEM((n_slabs - 1, 2, 2 * nj, lanes), f32),
            pltpu.VMEM((STEPS, max(nj // 2, 1), nk, lanes), f32),
            pltpu.VMEM((nj, ni, lanes), f32),
            pltpu.VMEM((nj, ni, lanes), f32),
            dma((parts,)),
            dma((parts,)),
            dma((parts,)),
            dma((STEPS, 2, nj)),
            dma((STEPS, 2, nj)),
            dma((STEPS, max(nj // 2, 1))),
            dma((STEPS, max(nj // 2, 1))),
            dma((STEPS, 2, parts + 2)),
            dma((STEPS, 2, parts + 2)),
            dma((STEPS, 2, 2)),
            dma((STEPS, 2, 2)),
            dma((STEPS, 2, parts + 2)),
            dma((STEPS, 2, parts + 2)),
            dma((STEPS, 2, 2)),
            dma((STEPS, 2, 2)),
            dma((parts, levels)),
            dma((parts, levels)),
            dma((n_slabs - 1,)),
            dma((n_slabs - 1,)),
        ],
        compiler_params=pltpu.CompilerParams(
            collective_id=0, has_side_effects=True, vmem_limit_bytes=40 * 2**20
        ),
        cost_estimate=pl.CostEstimate(flops=33 * cells, bytes_accessed=12 * cells, transcendentals=0),
    )(field_now, earlier, speed_square)
    return pl.pallas_call(
        finish_kernel,
        name="finish",
        out_shape=(jax.ShapeDtypeStruct(field_now.shape, f32),) * 2,
        in_specs=[vmem] * 4,
        out_specs=(hbm,) * 2,
        scratch_shapes=[
            pltpu.VMEM((2, nj, nk, lanes), f32),
            dma((nj,)),
            dma((nj,)),
            dma((2,)),
        ],
        compiler_params=pltpu.CompilerParams(vmem_limit_bytes=16 * 2**20),
        cost_estimate=pl.CostEstimate(flops=2 * cells, bytes_accessed=8 * cells, transcendentals=0),
    )(field, scaled, mean, scale)


def crosses(mesh):
    order = ("rows", "cols", "slabs")
    devices = mesh.devices.transpose([mesh.axis_names.index(axis) for axis in order])
    if devices.shape[1] != 4:
        return False
    one, other = (getattr(devices[0, place, 0], "coords", None) for place in (1, 2))
    return one is not None and sum(a != b for a, b in zip(one, other)) > 1


def solution(mesh):
    spec = P("rows", "cols", "slabs", None)
    return jax.shard_map(
        functools.partial(shards, dict(mesh.shape), crosses(mesh)),
        mesh=mesh,
        in_specs=(spec,) * 3,
        out_specs=(spec,) * 2,
        check_vma=False,
    )
```

time: 51.8 us -> 48.9 us (0.944)
  Pallas kernels: 51 us -> 48.1 us
    pallas_call x1, Pallas kernels: 45 us -> 42.2 us  [shards(): pl.pallas_call(functools.partial(march_kernel, counts, relay), name='marc...]
where the time goes in v1:
time: 48.9 us; the launch traced here: 48.8 us
  Pallas kernels  48.1 us (98%)
  between operations  0.64 us (1%)
    pallas_call x1, Pallas kernels, shards(): pl.pallas_call(functools.partial(march_kernel, counts, relay), name='marc...  42.2 us
    pallas_call x1, Pallas kernels, shards(): pl.pallas_call(finish_kernel, name='finish', out_shape=(jax.ShapeDtypeStr...  5.93 us

profile of v1, /device:TPU:0, one launch (start us, length us, event | category | flops | bytes accessed | tf_op | source)
XLA Modules:
  0.0 48.8 jit_solution(845599984470027274)
XLA Ops:
  0.6 42.2 %march.1 = (f32[6,34,128,128]{3,2,1,0:T(8,128)S(1)}, f32[4,32,128,128]{3,2,1,0:T(8,128)S(1)}, f32[8,128]{1,0:T(8,128)S(1)}, f32[8,128]{1,0:T(8,128)S(1)}) custom-call(f32[4,32,128,128]{3,2,1,0:T(8,128)} %now_hbm.1, f32[4,32,128,128]{3,2,1,0:T(8,128)} %old_hbm.1, f32[4,32,128,128]{3,2,1,0:T(8,128)} %speed_hbm.1), custom_call_target="tpu_custom_call" | custom-call | flops 69206016 | bytes 25165824 | tf_op jit(solution)/shard_map/march/pallas_call | solution.py:561
  42.9 5.9 %finish.1 = (f32[4,32,128,128]{3,2,1,0:T(8,128)}, f32[4,32,128,128]{3,2,1,0:T(8,128)}) custom-call(f32[6,34,128,128]{3,2,1,0:T(8,128)S(1)} %get-tuple-element.6.field, f32[4,32,128,128]{3,2,1,0:T(8,128)S(1)} %get-tuple-element.7.scaled, f32[8,128]{1,0:T(8,128)S(1)} %get-tuple-element.8.mean_ref, f32[8,128]{1,0:T(8,128)S(1)} %get-tuple-element.9.scale_ref), custom_call_target="tpu_custom_call" | custom-call | flops 4194304 | bytes 16777216 | tf_op jit(solution)/shard_map/finish/pallas_call | solution.py:610

commit v2 on v1

v2 whole, which is shorter than its diff:
```python
import functools

import jax
import jax.numpy as jnp
from jax import lax
from jax.experimental import pallas as pl
from jax.experimental.pallas import tpu as pltpu
from jax.sharding import PartitionSpec as P

STEPS = 3
EPS = 1e-4
MESH = pl.DeviceIdType.MESH
AXES = ("rows", "cols", "slabs")
OWN, DIAG = 0, 1
FILL = ((6.7, 7.7, 8.9, 9.8), (10.6, 11.8, 12.6, 13.6), (15.6, 16.4, 17.7, 19.2))
PASS = ((7.2, 8.6), (15.3, 18.9), (24.5, 27.4))
EDGE = (
    ((8.65, 8.7, 11.4, 15.4), (11.7, 14.6, 11.5, 14.1)),
    ((16.3, 17.6, 19.1, 24.6), (20.6, 23.5, 21.4, 24.3)),
    ((25.0, 26.5, 28.0, 32.0), (29.5, 32.5, 30.3, 31.8)),
)
STRIPS = (15.5, 24.7)
STATS = (20.5, 24.8)
ADVANCE = (25.3, 28.2)


def line_parts(ni):
    return 4 if ni % 32 == 0 else 1


def edge_places(cols, ni):
    odd = lax.rem(cols, 2)
    return ni - odd * (ni - 1), 1 + odd * (ni - 1)


def march_kernel(
    counts, relay, now_hbm, old_hbm, speed_hbm, field, scaled, mean_ref, scale_ref,
    work, face_out, face_in, rim_out, rim_in, own_stats, own_edge, in_stats, all_edge, relayed,
    means, scales, load_x, load_y, load_c,
    side_send, side_recv, pass_send, pass_recv, row_send, row_recv, row_rim_send, row_rim_recv,
    slab_send, slab_recv, slab_rim_send, slab_rim_recv, stat_send, stat_recv, edge_send, edge_recv,
):
    nj, ni, nk, lanes = now_hbm.shape
    speed = scaled
    n_slabs = counts["slabs"]
    parts = line_parts(ni)
    width = ni // parts
    inside_out = [0, *range(parts - 1, 0, -1)]
    outside_in = inside_out[2:] + inside_out[:2]
    here = {axis: lax.axis_index(axis) for axis in AXES}
    has_low = {axis: here[axis] > 0 for axis in AXES}
    has_high = {axis: here[axis] < counts[axis] - 1 for axis in AXES}
    odd = lax.rem(here["cols"], 2)
    places = edge_places(here["cols"], ni)
    beside = (here["cols"] + 1 - 2 * odd, here["cols"] - 1 + 2 * odd)
    has_side = tuple((other >= 0) & (other < counts["cols"]) for other in beside)
    halos = ((1 - odd) * (ni + 1), odd * (ni + 1))

    def span(part):
        return part * width, (part + 1) * width

    def load(name, part):
        start, _ = span(part)
        plain, padded = pl.ds(start, width), (pl.ds(1, nj), pl.ds(1 + start, width))
        source, target, sem = {
            "now": (now_hbm, work.at[padded], load_x),
            "old": (old_hbm, field.at[padded], load_y),
            "speed": (speed_hbm, speed.at[:, plain], load_c),
        }[name]
        return pltpu.make_async_copy(source.at[:, plain], target, sem.at[part])

    for part in inside_out:
        load("now", part).start()
    for part in inside_out[:2]:
        load("old", part).start()
        load("speed", part).start()

    barrier = pltpu.get_barrier_semaphore()
    expected = jnp.int32(0)
    for axis in AXES:
        for there, shift in ((has_low[axis], -1), (has_high[axis], 1)):
            expected = expected + there.astype(jnp.int32)

            @pl.when(there)
            def _():
                pl.semaphore_signal(barrier, inc=1, device_id={axis: here[axis] + shift}, device_id_type=MESH)

    peers = [lax.rem(here["slabs"] + gap, n_slabs) for gap in range(1, n_slabs)]
    if relay:
        over = lax.rem(here["cols"] + 2, 4)
        pl.semaphore_signal(barrier, inc=1, device_id={"cols": over}, device_id_type=MESH)
        expected = expected + 1
    pl.semaphore_wait(barrier, expected)
    for part in inside_out[2:]:
        load("old", part).start()
        load("speed", part).start()

    half = nj // 2 if relay else 0
    relays = has_side[OWN] & ~has_side[DIAG]

    def buffer_of(step):
        return work if step % 2 == 0 else field

    def remote(source, landing, send, recv, axis, target):
        return pltpu.make_async_remote_copy(
            source, landing, send, recv, device_id={axis: target}, device_id_type=MESH
        )

    def directions(axis):
        for to_high in (0, 1):
            yield to_high, has_high[axis] if to_high else has_low[axis], here[axis] + (1 if to_high else -1)

    def taken(axis, one, two):
        pl.when(has_low[axis] & has_high[axis])(two.wait_recv)
        pl.when(has_low[axis] ^ has_high[axis])(one.wait_recv)

    def side_copy(step, which, j, kind="straight"):
        buffer = buffer_of(step)
        source, target = buffer.at[j + 1, places[which]], beside[which]
        landing = buffer.at[j + 1, ni + 1 - halos[which]]
        sems = side_send.at[step % 2, which], side_recv.at[step % 2, which, j]
        if kind == "to":
            landing, target = relayed.at[step, j], over
            sems = sems[0], pass_recv.at[step % 2, j]
        elif kind == "on":
            source, landing, target = relayed.at[step, j], buffer.at[j + 1, halos[OWN]], beside[OWN]
            sems = pass_send, sems[1]
        return remote(source, landing, *sems, "cols", target)

    def side(step, which, j, what):
        relayed_line = which == DIAG and j < half
        if what == "start":
            pl.when(has_side[which])(side_copy(step, which, j, "to" if relayed_line else "straight").start)
        else:
            pl.when(has_side[which])(side_copy(step, which, j).wait_recv)

    def side_sent(step, which):
        lines = buffer_of(step).at[pl.ds(1, nj), places[which]]
        copy = remote(lines, lines, side_send.at[step % 2, which], side_recv.at[step % 2, which, 0], "cols", beside[which])
        pl.when(has_side[which])(copy.wait_send)

    def hand_on(step, j):
        @pl.when(relays)
        def _():
            side_copy(step, DIAG, j, "to").wait_recv()
            side_copy(step, DIAG, j, "on").start()

    def segment(step, number):
        if number < parts:
            start, stop = span(number)
            rim = 1 if step < 2 else 2
            return max(1 + start, 1 + rim), min(1 + stop, 1 + ni - rim)
        place = 2 if number == parts else ni - 1
        return place, place + 1

    def slot(step, number):
        return step % 2 * parts + number if number < parts else parts + number

    def rows(step, number, what):
        start, stop = segment(step, number)
        lines, buffer, recv = pl.ds(start, stop - start), buffer_of(step), row_recv.at[slot(step, number)]
        if what == "taken":
            one, two = (buffer.at[pl.ds(0, n), lines] for n in (1, 2))
            send = row_send.at[step % 2, 0]
            taken("rows", *(remote(some, some, send, recv, "rows", here["rows"]) for some in (one, two)))
            return
        for to_high, there, target in directions("rows"):
            source, landing = (nj, 0) if to_high else (1, nj + 1)
            copy = remote(
                buffer.at[source, lines], buffer.at[landing, lines], row_send.at[step % 2, to_high], recv, "rows", target
            )
            pl.when(there)(copy.start)

    def rows_sent(step):
        for to_high, there, target in directions("rows"):
            lines = buffer_of(step).at[nj if to_high else 1, pl.ds(2, ni - 2)]
            copy = remote(lines, lines, row_send.at[step % 2, to_high], row_recv.at[0], "rows", target)
            pl.when(there)(copy.wait_send)

    def row_rim(step, which, to_highs, what):
        buffer = buffer_of(step)
        for to_high, there, target in directions("rows"):
            if to_high not in to_highs:
                continue
            source, landing = (nj, 0) if to_high else (1, nj + 1)
            copy = remote(
                buffer.at[source, places[which]], buffer.at[landing, places[which]],
                row_rim_send.at[step % 2, to_high], row_rim_recv.at[step % 2, to_high, which], "rows", target,
            )
            if what == "start":
                pl.when(there)(copy.start)
            else:
                pl.when(has_low["rows"] if to_high else has_high["rows"])(copy.wait_recv)

    def row_rim_sent(step):
        for to_high, there, target in directions("rows"):
            lines = buffer_of(step).at[nj if to_high else 1, pl.ds(1, 2)]
            copy = remote(
                lines, lines, row_rim_send.at[step % 2, to_high], row_rim_recv.at[0, to_high, 0], "rows", target
            )
            pl.when(there)(copy.wait_send)

    def slabs(step, number, what):
        start, stop = segment(step, number)
        lines, recv = pl.ds(start - 1, stop - start), slab_recv.at[slot(step, number)]
        if what == "taken":
            one, two = (face_in.at[step, pl.ds(0, n), lines] for n in (1, 2))
            taken("slabs", *(remote(some, some, slab_send.at[0], recv, "slabs", here["slabs"]) for some in (one, two)))
            return
        for to_high, there, target in directions("slabs"):
            copy = remote(
                face_out.at[step, to_high, lines], face_in.at[step, to_high, lines],
                slab_send.at[to_high], recv, "slabs", target,
            )
            pl.when(there)(copy.start)

    def slab_rim(step, which, j, what):
        recv = slab_rim_recv.at[step % 2, which, j]
        if what == "taken":
            one, two = (rim_in.at[step, pl.ds(0, n), which, j] for n in (1, 2))
            taken("slabs", *(remote(some, some, slab_rim_send.at[0], recv, "slabs", here["slabs"]) for some in (one, two)))
            return
        for to_high, there, target in directions("slabs"):
            copy = remote(
                rim_out.at[step, to_high, which, j], rim_in.at[step, to_high, which, j],
                slab_rim_send.at[to_high], recv, "slabs", target,
            )
            pl.when(there)(copy.start)

    def slabs_sent():
        for to_high, there, target in directions("slabs"):
            faces, rims = face_out.at[:, to_high, pl.ds(1, ni - 2)], rim_out.at[:, to_high]
            pl.when(there)(remote(faces, faces, slab_send.at[to_high], slab_recv.at[0], "slabs", target).wait_send)
            copy = remote(rims, rims, slab_rim_send.at[to_high], slab_rim_recv.at[0, 0, 0], "slabs", target)
            pl.when(there)(copy.wait_send)

    for part in inside_out[:2]:
        load("now", part).wait()
    for j in range(half):
        side(0, DIAG, j, "start")
    first_sends, late_sends = opening(nj, half)
    for which, j in first_sends:
        side(0, which, j, "start")
    for which in (OWN, DIAG):
        for j in range(nj):
            rim_out[0, 0, which, j] = work[j + 1, places[which], pl.ds(0, 1), :]
            rim_out[0, 1, which, j] = work[j + 1, places[which], pl.ds(nk - 1, 1), :]
    for which in (OWN, DIAG):
        row_rim(0, which, (0, 1), "start")
        for j in range(nj):
            slab_rim(0, which, j, "start")

    zeros_line = jnp.zeros((nk, lanes), jnp.float32)
    for buffer in (work, field):
        for absent, edge in ((~has_low["rows"], 0), (~has_high["rows"], nj + 1)):
            @pl.when(absent)
            def _():
                @pl.loop(1, ni + 1)
                def _(i):
                    buffer[edge, i] = zeros_line
        for absent, edge in ((~has_low["cols"], 0), (~has_high["cols"], ni + 1)):
            @pl.when(absent)
            def _():
                @pl.loop(1, nj + 1)
                def _(j):
                    buffer[j, edge] = zeros_line
    for absent, to_high in ((~has_low["slabs"], 1), (~has_high["slabs"], 0)):
        @pl.when(absent)
        def _():
            for step in range(STEPS):
                face_in[step, to_high] = jnp.zeros((ni, nj, lanes), jnp.float32)
                rim_in[step, to_high] = jnp.zeros((2, nj, 1, lanes), jnp.float32)
    own_stats[...] = jnp.zeros_like(own_stats)

    for part in inside_out:
        if part not in inside_out[:2]:
            load("now", part).wait()
        rows(0, part, "start")
        start, stop = segment(0, part)

        @pl.loop(start, stop)
        def _(i):
            for j in range(nj):
                face_out[0, 0, i - 1, pl.ds(j, 1), :] = work[j + 1, i, pl.ds(0, 1), :]
                face_out[0, 1, i - 1, pl.ds(j, 1), :] = work[j + 1, i, pl.ds(nk - 1, 1), :]

        slabs(0, part, "start")

    groups = nk // 8
    row_number = lax.broadcasted_iota(jnp.int32, (8, lanes), 0)

    def line(step, i, js, rim=None):
        now, old = (work, field) if step % 2 == 1 else (field, work)
        last = step == STEPS
        sums = {}

        def halo(to_high, j):
            if rim is None:
                return face_in[step - 1, to_high, i - 1, pl.ds(j, 1), :]
            return rim_in[step - 1, to_high, rim, j]

        def keep(to_high, j, row):
            if rim is None:
                face_out[step, to_high, i - 1, pl.ds(j, 1), :] = row
            else:
                rim_out[step, to_high, rim, j] = row

        for g in range(groups):
            k = pl.ds(8 * g, 8)
            column = {j: now[j, i, k, :] for j in range(js[0], js[-1] + 3)}
            for j in js:
                middle = column[j + 1]
                if g == 0:
                    low = jnp.where(
                        row_number == 0, jnp.broadcast_to(halo(1, j), (8, lanes)), pltpu.roll(middle, 1, 0)
                    )
                else:
                    low = now[j + 1, i, pl.ds(8 * g - 1, 8), :]
                if g == groups - 1:
                    high = jnp.where(
                        row_number == 7, jnp.broadcast_to(halo(0, j), (8, lanes)), pltpu.roll(middle, 7, 0)
                    )
                else:
                    high = now[j + 1, i, pl.ds(8 * g + 1, 8), :]
                spread = (
                    (column[j] + column[j + 2])
                    + (now[j + 1, i - 1, k, :] + now[j + 1, i + 1, k, :])
                    + (low + high)
                    - 6.0 * middle
                )
                later = 2.0 * middle - old[j + 1, i, k, :] + speed[j, i - 1, k, :] * spread
                old[j + 1, i, k, :] = later
                if last:
                    sums[j] = later if g == 0 else sums[j] + later
                else:
                    if g == 0:
                        keep(0, j, later[0:1])
                    if g == groups - 1:
                        keep(1, j, later[7:8])
        if last:
            for j in js:
                total = jnp.sum(sums[j], axis=0, keepdims=True)
                mean = jnp.broadcast_to(total * (1.0 / nk), (8, lanes))
                squares = None
                for g in range(groups):
                    moved = old[j + 1, i, pl.ds(8 * g, 8), :] - mean
                    squares = moved * moved if g == 0 else squares + moved * moved
                square = jnp.sum(squares, axis=0, keepdims=True)
                if rim is None:
                    own_stats[0, 0, j, pl.ds(i - 1, 1), :] = total
                    own_stats[0, 1, j, pl.ds(i - 1, 1), :] = square
                else:
                    own_edge[0, pl.ds(rim * nj + j, 1), :] = total
                    own_edge[1, pl.ds(rim * nj + j, 1), :] = square

    every_j, begun = tuple(range(nj)), set()

    def interior(step, part):
        start, stop = span(part)
        rim = max(step, 1)
        start, stop = max(1 + start, 1 + rim), min(1 + stop, 1 + ni - rim)
        if step == 1:
            load("old", part).wait()
            load("speed", part).wait()
        rows(step - 1, part, "taken")
        slabs(step - 1, part, "taken")
        if step >= 2 and step not in begun:
            begun.add(step)
            rows_sent(step - 2)

        @pl.loop(start, stop)
        def _(i):
            line(step, i, every_j)

        if step < STEPS:
            rows(step, part, "start")
            slabs(step, part, "start")

    def strips(step):
        if step == 2:
            for number, place in ((parts, 2), (parts + 1, ni - 1)):
                line(step, place, every_j)
                rows(step, number, "start")
                slabs(step, number, "start")
        else:
            for number in (parts, parts + 1):
                rows(step - 1, number, "taken")
                slabs(step - 1, number, "taken")
            for place in (3, ni - 2, 2, ni - 1):
                line(step, place, every_j)

    def edge(step, which, j):
        side(step - 1, which, j, "taken")
        slab_rim(step - 1, which, j, "taken")
        shared = [to_high for to_high, place in ((0, 0), (1, nj - 1)) if place == j]
        row_rim(step - 1, which, [1 - to_high for to_high in shared], "taken")
        if step >= 2 and (step, which) not in begun:
            begun.add((step, which))
            side_sent(step - 2, which)
            if (step, OWN + DIAG - which) not in begun:
                row_rim_sent(step - 2)
        line(step, places[which], (j,), which)
        if step < STEPS:
            side(step, which, j, "start")
            slab_rim(step, which, j, "start")
            row_rim(step, which, shared, "start")

    levels = n_slabs.bit_length() - 1
    partners = []
    for level in range(levels):
        bit = lax.rem(here["slabs"] // 2**level, 2)
        partners.append(here["slabs"] + (1 - 2 * bit) * 2**level)

    def stat_copy(part, level):
        lines = pl.ds(part * width, width)
        return remote(
            own_stats.at[level, :, :, lines], in_stats.at[level, :, :, lines],
            stat_send, stat_recv.at[part, level], "slabs", partners[level],
        )

    def merged(part, level):
        lines = pl.ds(part * width, width)
        stat_copy(part, level).wait_recv()
        mine, theirs = own_stats[level, :, :, lines, :], in_stats[level, :, :, lines, :]
        cells = float(nk * 2**level)
        apart = (theirs[0] - mine[0]) * (1.0 / cells)
        return mine[0] + theirs[0], mine[1] + theirs[1] + (0.5 * cells) * apart * apart

    def advance(part, level):
        lines = pl.ds(part * width, width)
        total, square = merged(part, level)
        own_stats[level + 1, 0, :, lines, :] = total
        own_stats[level + 1, 1, :, lines, :] = square
        stat_copy(part, level + 1).start()

    whole = float(nk * n_slabs)

    def rescale(part):
        lines = pl.ds(part * width, width)
        total, square = merged(part, levels - 1)
        means[:, lines, :] = total * (1.0 / whole)
        scales[:, lines, :] = lax.rsqrt(square * (1.0 / whole) + EPS)
        start, stop = span(part)

        @pl.loop(max(start, 1), min(stop, ni - 1))
        def _(i):
            for j in range(nj):
                mean = jnp.broadcast_to(means[j, pl.ds(i, 1), :], (8, lanes))
                scale = jnp.broadcast_to(scales[j, pl.ds(i, 1), :], (8, lanes))
                for g in range(groups):
                    k = pl.ds(8 * g, 8)
                    scaled[j, i, k, :] = (field[j + 1, i + 1, k, :] - mean) * scale

    def do(kind, *what):
        if kind == "in":
            interior(what[0], what[1])
        elif kind == "own":
            edge(what[0], OWN, what[1])
        elif kind == "diag":
            edge(what[0], DIAG, what[1])
        elif kind == "pass":
            hand_on(*what)
        elif kind == "late":
            for which, j in late_sends:
                side(0, which, j, "start")
        elif kind == "strips":
            strips(what[0])
        elif kind == "stats":
            stat_copy(what[0], 0).start()
        elif kind == "advance":
            for level in range(levels - 1):
                advance(what[0], level)
        elif kind == "rescale":
            rescale(what[0])

    for what in agenda(nj, half, parts, inside_out, outside_in):
        do(*what)

    gaps = range(1, n_slabs)
    for gap in gaps:
        remote(own_edge, all_edge.at[gap - 1], edge_send, edge_recv, "slabs", peers[gap - 1]).start()
    for part in outside_in:
        rescale(part)

    def combine(own, others):
        mean = own[0]
        for other in others:
            mean = mean + other[0]
        mean = mean * (1.0 / whole)
        square = None
        for one in (own, *others):
            gap = one[0] * (1.0 / nk) - mean
            term = one[1] + nk * gap * gap
            square = term if square is None else square + term
        return mean, lax.rsqrt(square * (1.0 / whole) + EPS)

    for step in range(STEPS):
        if step == 2:
            for which in (OWN, DIAG):
                side_sent(step, which)
            row_rim_sent(step)
            rows_sent(step)
    slabs_sent()
    if half:
        pl.when(relays)(remote(relayed, relayed, pass_send, pass_recv.at[0, 0], "cols", beside[OWN]).wait_send)
    remote(own_stats, in_stats, stat_send, stat_recv.at[0, 0], "slabs", partners[0]).wait_send()
    edges = remote(all_edge, all_edge, edge_send, edge_recv, "slabs", peers[0])
    edges.wait_recv()
    mean, scale = combine(own_edge[...], [all_edge[gap - 1] for gap in gaps])
    mean_ref[...] = mean
    scale_ref[...] = scale
    edges.wait_send()


def opening(nj, half):
    own, diag = [(OWN, j) for j in range(nj)], [(DIAG, j) for j in range(half, nj)]
    woven = [(OWN, j) for j in range(nj - len(diag))]
    for late, line in zip(own[nj - len(diag):], diag):
        woven += [line, late]
    return woven[:-2], woven[-2:]


def agenda(nj, half, parts, first, last):
    timed = []

    def spread(times, entries):
        for n, entry in enumerate(entries):
            spot = (n + 0.5) / len(entries) * len(times) - 0.5
            low = min(max(int(spot), 0), len(times) - 1)
            high = min(low + 1, len(times) - 1)
            timed.append((times[low] + (spot - low) * (times[high] - times[low]), len(timed), entry))

    own = {step: [("own", step, n) for n in range(nj)] for step in range(1, STEPS + 1)}
    diag = {step: [("diag", step, n) for n in range(nj)] for step in range(1, STEPS + 1)}
    passes = [[("pass", step, j) for j in range(half)] for step in range(STEPS)]
    spread(FILL[0], [("in", 1, part) for part in first])
    spread(FILL[1], [("in", 2, part) for part in first])
    spread(FILL[2], [("in", 3, part) for part in first])
    for step in range(STEPS):
        spread(PASS[step], passes[step])
        spread(EDGE[step][OWN], own[step + 1])
        spread(EDGE[step][DIAG], diag[step + 1])
    spread([7.25], [("late",)])
    spread([STRIPS[0]], [("strips", 2)])
    spread([STRIPS[1]], [("strips", 3)])
    for n, part in enumerate(last):
        rim = part in (0, parts - 1)
        spread([STATS[rim] + 0.01 * n], [("stats", part)])
        spread([ADVANCE[rim] + 0.01 * n], [("advance", part)])
    return [entry for _, _, entry in sorted(timed, key=lambda spot: spot[:2])]


def finish_kernel(field, scaled, mean_ref, scale_ref, scaled_hbm, field_hbm, rims, field_sem, scaled_sem):
    nj, ni, nk, lanes = scaled_hbm.shape
    inner = pl.ds(1, ni - 2)
    for j in range(nj):
        pltpu.make_async_copy(field.at[j + 1, pl.ds(1, ni)], field_hbm.at[j], field_sem).start()
        pltpu.make_async_copy(scaled.at[j, inner], scaled_hbm.at[j, inner], scaled_sem).start()
    places = edge_places(lax.axis_index("cols"), ni)
    for which in (OWN, DIAG):
        for j in range(nj):
            row = pl.ds(which * nj + j, 1)
            mean = jnp.broadcast_to(mean_ref[row, :], (8, lanes))
            scale = jnp.broadcast_to(scale_ref[row, :], (8, lanes))
            for g in range(nk // 8):
                k = pl.ds(8 * g, 8)
                rims[which, j, k, :] = (field[j + 1, places[which], k, :] - mean) * scale
        pltpu.make_async_copy(rims.at[which], scaled_hbm.at[:, places[which] - 1], scaled_sem).start()
    pltpu.make_async_copy(scaled, scaled_hbm, scaled_sem).wait()
    pltpu.make_async_copy(field.at[pl.ds(1, nj), pl.ds(1, ni)], field_hbm, field_sem).wait()


def shards(counts, relay, field_now, earlier, speed_square):
    nj, ni, nk, lanes = field_now.shape
    n_slabs = counts["slabs"]
    levels = n_slabs.bit_length() - 1
    assert n_slabs == 2**levels and levels >= 1
    relay = relay and nj > 1
    parts = line_parts(ni)
    f32 = jnp.float32
    padded = (nj + 2, ni + 2, nk, lanes)
    hbm = pl.BlockSpec(memory_space=pltpu.HBM)
    vmem = pl.BlockSpec(memory_space=pltpu.VMEM)
    cells = nj * ni * nk * lanes
    dma = pltpu.SemaphoreType.DMA
    field, scaled, mean, scale = pl.pallas_call(
        functools.partial(march_kernel, counts, relay),
        name="march",
        out_shape=(
            pltpu.VMEM(padded, f32),
            pltpu.VMEM((nj, ni, nk, lanes), f32),
            pltpu.VMEM((2 * nj, lanes), f32),
            pltpu.VMEM((2 * nj, lanes), f32),
        ),
        in_specs=[hbm] * 3,
        out_specs=(vmem,) * 4,
        scratch_shapes=[
            pltpu.VMEM(padded, f32),
            pltpu.VMEM((STEPS, 2, ni, nj, lanes), f32),
            pltpu.VMEM((STEPS, 2, ni, nj, lanes), f32),
            pltpu.VMEM((STEPS, 2, 2, nj, 1, lanes), f32),
            pltpu.VMEM((STEPS, 2, 2, nj, 1, lanes), f32),
            pltpu.VMEM((levels, 2, nj, ni, lanes), f32),
            pltpu.VMEM((2, 2 * nj, lanes), f32),
            pltpu.VMEM((levels, 2, nj, ni, lanes), f32),
            pltpu.VMEM((n_slabs - 1, 2, 2 * nj, lanes), f32),
            pltpu.VMEM((STEPS, max(nj // 2, 1), nk, lanes), f32),
            pltpu.VMEM((nj, ni, lanes), f32),
            pltpu.VMEM((nj, ni, lanes), f32),
            dma((parts,)),
            dma((parts,)),
            dma((parts,)),
            dma((2, 2)),
            dma((2, 2, nj)),
            dma(()),
            dma((2, max(nj // 2, 1))),
            dma((2, 2)),
            dma((2 * parts + 2,)),
            dma((2, 2)),
            dma((2, 2, 2)),
            dma((2,)),
            dma((2 * parts + 2,)),
            dma((2,)),
            dma((2, 2, nj)),
            dma(()),
            dma((parts, levels)),
            dma(()),
            dma(()),
        ],
        compiler_params=pltpu.CompilerParams(
            collective_id=0, has_side_effects=True, vmem_limit_bytes=40 * 2**20
        ),
        cost_estimate=pl.CostEstimate(flops=33 * cells, bytes_accessed=12 * cells, transcendentals=0),
    )(field_now, earlier, speed_square)
    return pl.pallas_call(
        finish_kernel,
        name="finish",
        out_shape=(jax.ShapeDtypeStruct(field_now.shape, f32),) * 2,
        in_specs=[vmem] * 4,
        out_specs=(hbm,) * 2,
        scratch_shapes=[
            pltpu.VMEM((2, nj, nk, lanes), f32),
            dma(()),
            dma(()),
        ],
        compiler_params=pltpu.CompilerParams(vmem_limit_bytes=16 * 2**20),
        cost_estimate=pl.CostEstimate(flops=2 * cells, bytes_accessed=8 * cells, transcendentals=0),
    )(field, scaled, mean, scale)


def crosses(mesh):
    order = ("rows", "cols", "slabs")
    devices = mesh.devices.transpose([mesh.axis_names.index(axis) for axis in order])
    if devices.shape[1] != 4:
        return False
    one, other = (getattr(devices[0, place, 0], "coords", None) for place in (1, 2))
    return one is not None and sum(a != b for a, b in zip(one, other)) > 1


def solution(mesh):
    spec = P("rows", "cols", "slabs", None)
    return jax.shard_map(
        functools.partial(shards, dict(mesh.shape), crosses(mesh)),
        mesh=mesh,
        in_specs=(spec,) * 3,
        out_specs=(spec,) * 2,
        check_vma=False,
    )
```

time: 48.9 us -> 44.2 us (0.904)
  Pallas kernels: 48.1 us -> 43.3 us
    pallas_call x1, Pallas kernels: 42.2 us -> 37.5 us  [shards(): pl.pallas_call(functools.partial(march_kernel, counts, relay), name='marc...]
where the time goes in v2:
time: 44.2 us; the launch traced here: 44 us
  Pallas kernels  43.3 us (98%)
  between operations  0.64 us (1%)
    pallas_call x1, Pallas kernels, shards(): pl.pallas_call(functools.partial(march_kernel, counts, relay), name='marc...  37.5 us
    pallas_call x1, Pallas kernels, shards(): pl.pallas_call(finish_kernel, name='finish', out_shape=(jax.ShapeDtypeStr...  5.86 us

profile of v2, /device:TPU:0, one launch (start us, length us, event | category | flops | bytes accessed | tf_op | source)
XLA Modules:
  0.0 44.0 jit_solution(1702875785016933398)
XLA Ops:
  0.6 37.5 %march.1 = (f32[6,34,128,128]{3,2,1,0:T(8,128)S(1)}, f32[4,32,128,128]{3,2,1,0:T(8,128)S(1)}, f32[8,128]{1,0:T(8,128)S(1)}, f32[8,128]{1,0:T(8,128)S(1)}) custom-call(f32[4,32,128,128]{3,2,1,0:T(8,128)} %now_hbm.1, f32[4,32,128,128]{3,2,1,0:T(8,128)} %old_hbm.1, f32[4,32,128,128]{3,2,1,0:T(8,128)} %speed_hbm.1), custom_call_target="tpu_custom_call" | custom-call | flops 69206016 | bytes 25165824 | tf_op jit(solution)/shard_map/march/pallas_call | solution.py:586
  38.1 5.9 %finish.1 = (f32[4,32,128,128]{3,2,1,0:T(8,128)}, f32[4,32,128,128]{3,2,1,0:T(8,128)}) custom-call(f32[6,34,128,128]{3,2,1,0:T(8,128)S(1)} %get-tuple-element.6.field, f32[4,32,128,128]{3,2,1,0:T(8,128)S(1)} %get-tuple-element.7.scaled, f32[8,128]{1,0:T(8,128)S(1)} %get-tuple-element.8.mean_ref, f32[8,128]{1,0:T(8,128)S(1)} %get-tuple-element.9.scale_ref), custom_call_target="tpu_custom_call" | custom-call | flops 4194304 | bytes 16777216 | tf_op jit(solution)/shard_map/finish/pallas_call | solution.py:635

commit v3 on v2

--- a/solution.py
+++ b/solution.py
@@ -12,16 +12,16 @@
 MESH = pl.DeviceIdType.MESH
 AXES = ("rows", "cols", "slabs")
 OWN, DIAG = 0, 1
-FILL = ((6.7, 7.7, 8.9, 9.8), (10.6, 11.8, 12.6, 13.6), (15.6, 16.4, 17.7, 19.2))
-PASS = ((7.2, 8.6), (15.3, 18.9), (24.5, 27.4))
+FILL = ((6.7, 8.0, 8.8, 9.7), (10.5, 11.3, 12.5, 13.3), (14.2, 15.0, 16.3, 17.7))
+PASS = ((6.0, 7.4), (14.05, 17.1), (23.2, 26.0))
 EDGE = (
-    ((8.65, 8.7, 11.4, 15.4), (11.7, 14.6, 11.5, 14.1)),
-    ((16.3, 17.6, 19.1, 24.6), (20.6, 23.5, 21.4, 24.3)),
-    ((25.0, 26.5, 28.0, 32.0), (29.5, 32.5, 30.3, 31.8)),
+    ((7.65, 7.7, 8.75, 13.25), (10.2, 13.2, 12.45, 13.95)),
+    ((17.15, 17.2, 17.65, 22.95), (19.1, 22.1, 19.9, 22.9)),
+    ((23.6, 25.1, 26.6, 31.1), (28.1, 31.0, 28.9, 30.4)),
 )
-STRIPS = (15.5, 24.7)
-STATS = (20.5, 24.8)
-ADVANCE = (25.3, 28.2)
+STRIPS = (14.0, 23.0)
+STATS = (19.0, 23.05)
+ADVANCE = (23.15, 26.7)
 
 
 def line_parts(ni):
@@ -36,9 +36,9 @@
 def march_kernel(
     counts, relay, now_hbm, old_hbm, speed_hbm, field, scaled, mean_ref, scale_ref,
     work, face_out, face_in, rim_out, rim_in, own_stats, own_edge, in_stats, all_edge, relayed,
-    means, scales, load_x, load_y, load_c,
-    side_send, side_recv, pass_send, pass_recv, row_send, row_recv, row_rim_send, row_rim_recv,
-    slab_send, slab_recv, slab_rim_send, slab_rim_recv, stat_send, stat_recv, edge_send, edge_recv,
+    means, scales, load_rim, load_x, load_y, load_c,
+    side_send, side_recv, pass_send, pass_recv, row_send, row_recv, row_rim_recv,
+    slab_send, slab_recv, slab_rim_recv, stat_send, edge_send, edge_recv,
 ):
     nj, ni, nk, lanes = now_hbm.shape
     speed = scaled
@@ -60,8 +60,10 @@
         return part * width, (part + 1) * width
 
     def load(name, part):
-        start, _ = span(part)
-        plain, padded = pl.ds(start, width), (pl.ds(1, nj), pl.ds(1 + start, width))
+        start, stop = span(part)
+        if name == "now":
+            start, stop = max(start, 1), min(stop, ni - 1)
+        plain, padded = pl.ds(start, stop - start), (pl.ds(1, nj), pl.ds(1 + start, stop - start))
         source, target, sem = {
             "now": (now_hbm, work.at[padded], load_x),
             "old": (old_hbm, field.at[padded], load_y),
@@ -69,6 +71,8 @@
         }[name]
         return pltpu.make_async_copy(source.at[:, plain], target, sem.at[part])
 
+    for place in (0, ni - 1):
+        pltpu.make_async_copy(now_hbm.at[:, place], work.at[pl.ds(1, nj), place + 1], load_rim).start()
     for part in inside_out:
         load("now", part).start()
     for part in inside_out[:2]:
@@ -77,13 +81,15 @@
 
     barrier = pltpu.get_barrier_semaphore()
     expected = jnp.int32(0)
-    for axis in AXES:
-        for there, shift in ((has_low[axis], -1), (has_high[axis], 1)):
-            expected = expected + there.astype(jnp.int32)
-
-            @pl.when(there)
-            def _():
-                pl.semaphore_signal(barrier, inc=1, device_id={axis: here[axis] + shift}, device_id_type=MESH)
+    greeted = [("cols", has_side[which], beside[which]) for which in ((OWN,) if relay else (OWN, DIAG))]
+    for axis in ("rows", "slabs"):
+        greeted += [(axis, has_low[axis], here[axis] - 1), (axis, has_high[axis], here[axis] + 1)]
+    for axis, there, target in greeted:
+        expected = expected + there.astype(jnp.int32)
+
+        @pl.when(there)
+        def _():
+            pl.semaphore_signal(barrier, inc=1, device_id={axis: target}, device_id_type=MESH)
 
     peers = [lax.rem(here["slabs"] + gap, n_slabs) for gap in range(1, n_slabs)]
     if relay:
@@ -130,7 +136,9 @@
     def side(step, which, j, what):
         relayed_line = which == DIAG and j < half
         if what == "start":
-            pl.when(has_side[which])(side_copy(step, which, j, "to" if relayed_line else "straight").start)
+            held = half and which == OWN and j == nj - 1
+            there = has_side[which] & ~relays if held else has_side[which]
+            pl.when(there)(side_copy(step, which, j, "to" if relayed_line else "straight").start)
         else:
             pl.when(has_side[which])(side_copy(step, which, j).wait_recv)
 
@@ -144,6 +152,8 @@
         def _():
             side_copy(step, DIAG, j, "to").wait_recv()
             side_copy(step, DIAG, j, "on").start()
+            if j == 0:
+                side_copy(step, OWN, nj - 1).start()
 
     def segment(step, number):
         if number < parts:
@@ -173,7 +183,7 @@
 
     def rows_sent(step):
         for to_high, there, target in directions("rows"):
-            lines = buffer_of(step).at[nj if to_high else 1, pl.ds(2, ni - 2)]
+            lines = buffer_of(step).at[nj if to_high else 1, pl.ds(1, ni)]
             copy = remote(lines, lines, row_send.at[step % 2, to_high], row_recv.at[0], "rows", target)
             pl.when(there)(copy.wait_send)
 
@@ -185,20 +195,12 @@
             source, landing = (nj, 0) if to_high else (1, nj + 1)
             copy = remote(
                 buffer.at[source, places[which]], buffer.at[landing, places[which]],
-                row_rim_send.at[step % 2, to_high], row_rim_recv.at[step % 2, to_high, which], "rows", target,
+                row_send.at[step % 2, to_high], row_rim_recv.at[step % 2, to_high, which], "rows", target,
             )
             if what == "start":
                 pl.when(there)(copy.start)
             else:
                 pl.when(has_low["rows"] if to_high else has_high["rows"])(copy.wait_recv)
-
-    def row_rim_sent(step):
-        for to_high, there, target in directions("rows"):
-            lines = buffer_of(step).at[nj if to_high else 1, pl.ds(1, 2)]
-            copy = remote(
-                lines, lines, row_rim_send.at[step % 2, to_high], row_rim_recv.at[0, to_high, 0], "rows", target
-            )
-            pl.when(there)(copy.wait_send)
 
     def slabs(step, number, what):
         start, stop = segment(step, number)
@@ -218,29 +220,28 @@
         recv = slab_rim_recv.at[step % 2, which, j]
         if what == "taken":
             one, two = (rim_in.at[step, pl.ds(0, n), which, j] for n in (1, 2))
-            taken("slabs", *(remote(some, some, slab_rim_send.at[0], recv, "slabs", here["slabs"]) for some in (one, two)))
+            taken("slabs", *(remote(some, some, slab_send.at[0], recv, "slabs", here["slabs"]) for some in (one, two)))
             return
         for to_high, there, target in directions("slabs"):
             copy = remote(
                 rim_out.at[step, to_high, which, j], rim_in.at[step, to_high, which, j],
-                slab_rim_send.at[to_high], recv, "slabs", target,
+                slab_send.at[to_high], recv, "slabs", target,
             )
             pl.when(there)(copy.start)
 
     def slabs_sent():
         for to_high, there, target in directions("slabs"):
-            faces, rims = face_out.at[:, to_high, pl.ds(1, ni - 2)], rim_out.at[:, to_high]
-            pl.when(there)(remote(faces, faces, slab_send.at[to_high], slab_recv.at[0], "slabs", target).wait_send)
-            copy = remote(rims, rims, slab_rim_send.at[to_high], slab_rim_recv.at[0, 0, 0], "slabs", target)
-            pl.when(there)(copy.wait_send)
-
-    for part in inside_out[:2]:
-        load("now", part).wait()
+            sent = face_out.at[:, to_high]
+            pl.when(there)(remote(sent, sent, slab_send.at[to_high], slab_recv.at[0], "slabs", target).wait_send)
+
+    pltpu.make_async_copy(now_hbm.at[:, pl.ds(0, 2)], work.at[pl.ds(1, nj), pl.ds(1, 2)], load_rim).wait()
     for j in range(half):
         side(0, DIAG, j, "start")
-    first_sends, late_sends = opening(nj, half)
-    for which, j in first_sends:
-        side(0, which, j, "start")
+    for j in range(nj):
+        side(0, OWN, j, "start")
+    if not half:
+        for j in range(nj):
+            side(0, DIAG, j, "start")
     for which in (OWN, DIAG):
         for j in range(nj):
             rim_out[0, 0, which, j] = work[j + 1, places[which], pl.ds(0, 1), :]
@@ -273,8 +274,7 @@
     own_stats[...] = jnp.zeros_like(own_stats)
 
     for part in inside_out:
-        if part not in inside_out[:2]:
-            load("now", part).wait()
+        load("now", part).wait()
         rows(0, part, "start")
         start, stop = segment(0, part)
 
@@ -355,13 +355,18 @@
 
     every_j, begun = tuple(range(nj)), set()
 
+    def loaded(part):
+        if ("load", part) not in begun:
+            begun.add(("load", part))
+            load("old", part).wait()
+            load("speed", part).wait()
+
     def interior(step, part):
         start, stop = span(part)
         rim = max(step, 1)
         start, stop = max(1 + start, 1 + rim), min(1 + stop, 1 + ni - rim)
         if step == 1:
-            load("old", part).wait()
-            load("speed", part).wait()
+            loaded(part)
         rows(step - 1, part, "taken")
         slabs(step - 1, part, "taken")
         if step >= 2 and step not in begun:
@@ -397,15 +402,20 @@
         if step >= 2 and (step, which) not in begun:
             begun.add((step, which))
             side_sent(step - 2, which)
-            if (step, OWN + DIAG - which) not in begun:
-                row_rim_sent(step - 2)
+        if step == 1:
+            loaded(0)
+            loaded(parts - 1)
         line(step, places[which], (j,), which)
+        if half and (step, which, j) == (1, OWN, 0):
+            for other in range(half, nj):
+                side(0, DIAG, other, "start")
         if step < STEPS:
             side(step, which, j, "start")
             slab_rim(step, which, j, "start")
             row_rim(step, which, shared, "start")
 
     levels = n_slabs.bit_length() - 1
+    stat_recv = (load_x, load_y, load_c)
     partners = []
     for level in range(levels):
         bit = lax.rem(here["slabs"] // 2**level, 2)
@@ -415,7 +425,7 @@
         lines = pl.ds(part * width, width)
         return remote(
             own_stats.at[level, :, :, lines], in_stats.at[level, :, :, lines],
-            stat_send, stat_recv.at[part, level], "slabs", partners[level],
+            stat_send, stat_recv[level].at[part], "slabs", partners[level],
         )
 
     def merged(part, level):
@@ -460,9 +470,6 @@
             edge(what[0], DIAG, what[1])
         elif kind == "pass":
             hand_on(*what)
-        elif kind == "late":
-            for which, j in late_sends:
-                side(0, which, j, "start")
         elif kind == "strips":
             strips(what[0])
         elif kind == "stats":
@@ -498,12 +505,11 @@
         if step == 2:
             for which in (OWN, DIAG):
                 side_sent(step, which)
-            row_rim_sent(step)
             rows_sent(step)
     slabs_sent()
     if half:
         pl.when(relays)(remote(relayed, relayed, pass_send, pass_recv.at[0, 0], "cols", beside[OWN]).wait_send)
-    remote(own_stats, in_stats, stat_send, stat_recv.at[0, 0], "slabs", partners[0]).wait_send()
+    remote(own_stats, in_stats, stat_send, stat_recv[0].at[0], "slabs", partners[0]).wait_send()
     edges = remote(all_edge, all_edge, edge_send, edge_recv, "slabs", peers[0])
     edges.wait_recv()
     mean, scale = combine(own_edge[...], [all_edge[gap - 1] for gap in gaps])
@@ -512,21 +518,13 @@
     edges.wait_send()
 
 
-def opening(nj, half):
-    own, diag = [(OWN, j) for j in range(nj)], [(DIAG, j) for j in range(half, nj)]
-    woven = [(OWN, j) for j in range(nj - len(diag))]
-    for late, line in zip(own[nj - len(diag):], diag):
-        woven += [line, late]
-    return woven[:-2], woven[-2:]
-
-
 def agenda(nj, half, parts, first, last):
     timed = []
 
     def spread(times, entries):
         for n, entry in enumerate(entries):
-            spot = (n + 0.5) / len(entries) * len(times) - 0.5
-            low = min(max(int(spot), 0), len(times) - 1)
+            spot = min(max((n + 0.5) / len(entries) * len(times) - 0.5, 0), len(times) - 1)
+            low = int(spot)
             high = min(low + 1, len(times) - 1)
             timed.append((times[low] + (spot - low) * (times[high] - times[low]), len(timed), entry))
 
@@ -540,7 +538,6 @@
         spread(PASS[step], passes[step])
         spread(EDGE[step][OWN], own[step + 1])
         spread(EDGE[step][DIAG], diag[step + 1])
-    spread([7.25], [("late",)])
     spread([STRIPS[0]], [("strips", 2)])
     spread([STRIPS[1]], [("strips", 3)])
     for n, part in enumerate(last):
@@ -574,7 +571,7 @@
     nj, ni, nk, lanes = field_now.shape
     n_slabs = counts["slabs"]
     levels = n_slabs.bit_length() - 1
-    assert n_slabs == 2**levels and levels >= 1
+    assert n_slabs == 2**levels and 1 <= levels <= 3
     relay = relay and nj > 1
     parts = line_parts(ni)
     f32 = jnp.float32
@@ -607,6 +604,7 @@
             pltpu.VMEM((STEPS, max(nj // 2, 1), nk, lanes), f32),
             pltpu.VMEM((nj, ni, lanes), f32),
             pltpu.VMEM((nj, ni, lanes), f32),
+            dma(()),
             dma((parts,)),
             dma((parts,)),
             dma((parts,)),
@@ -616,14 +614,11 @@
             dma((2, max(nj // 2, 1))),
             dma((2, 2)),
             dma((2 * parts + 2,)),
-            dma((2, 2)),
             dma((2, 2, 2)),
             dma((2,)),
             dma((2 * parts + 2,)),
-            dma((2,)),
             dma((2, 2, nj)),
             dma(()),
-            dma((parts, levels)),
             dma(()),
             dma(()),
         ],

time: 44.2 us -> 43 us (0.973)
  Pallas kernels: 43.3 us -> 42.3 us
    pallas_call x1, Pallas kernels: 37.5 us -> 36.4 us  [shards(): pl.pallas_call(functools.partial(march_kernel, counts, relay), name='marc...]
where the time goes in v3:
time: 43 us; the launch traced here: 42.9 us
  Pallas kernels  42.3 us (98%)
  between operations  0.64 us (1%)
    pallas_call x1, Pallas kernels, shards(): pl.pallas_call(functools.partial(march_kernel, counts, relay), name='marc...  36.4 us
    pallas_call x1, Pallas kernels, shards(): pl.pallas_call(finish_kernel, name='finish', out_shape=(jax.ShapeDtypeStr...  5.86 us

profile of v3, /device:TPU:0, one launch (start us, length us, event | category | flops | bytes accessed | tf_op | source)
XLA Modules:
  0.0 42.9 jit_solution(5407919996227446733)
XLA Ops:
  0.6 36.4 %march.1 = (f32[6,34,128,128]{3,2,1,0:T(8,128)S(1)}, f32[4,32,128,128]{3,2,1,0:T(8,128)S(1)}, f32[8,128]{1,0:T(8,128)S(1)}, f32[8,128]{1,0:T(8,128)S(1)}) custom-call(f32[4,32,128,128]{3,2,1,0:T(8,128)} %now_hbm.1, f32[4,32,128,128]{3,2,1,0:T(8,128)} %old_hbm.1, f32[4,32,128,128]{3,2,1,0:T(8,128)} %speed_hbm.1), custom_call_target="tpu_custom_call" | custom-call | flops 69206016 | bytes 25165824 | tf_op jit(solution)/shard_map/march/pallas_call | solution.py:583
  37.0 5.9 %finish.1 = (f32[4,32,128,128]{3,2,1,0:T(8,128)}, f32[4,32,128,128]{3,2,1,0:T(8,128)}) custom-call(f32[6,34,128,128]{3,2,1,0:T(8,128)S(1)} %get-tuple-element.6.field, f32[4,32,128,128]{3,2,1,0:T(8,128)S(1)} %get-tuple-element.7.scaled, f32[8,128]{1,0:T(8,128)S(1)} %get-tuple-element.8.mean_ref, f32[8,128]{1,0:T(8,128)S(1)} %get-tuple-element.9.scale_ref), custom_call_target="tpu_custom_call" | custom-call | flops 4194304 | bytes 16777216 | tf_op jit(solution)/shard_map/finish/pallas_call | solution.py:630

commit v4 on v3

--- a/solution.py
+++ b/solution.py
@@ -16,12 +16,12 @@
 PASS = ((6.0, 7.4), (14.05, 17.1), (23.2, 26.0))
 EDGE = (
     ((7.65, 7.7, 8.75, 13.25), (10.2, 13.2, 12.45, 13.95)),
-    ((17.15, 17.2, 17.65, 22.95), (19.1, 22.1, 19.9, 22.9)),
-    ((23.6, 25.1, 26.6, 31.1), (28.1, 31.0, 28.9, 30.4)),
+    ((17.15, 17.2, 17.65, 19.5), (19.1, 22.1, 19.9, 22.9)),
+    ((23.6, 25.1, 26.6, 29.5), (28.1, 31.0, 30.3, 31.8)),
 )
 STRIPS = (14.0, 23.0)
 STATS = (19.0, 23.05)
-ADVANCE = (23.15, 26.7)
+ADVANCE = (23.7, 26.7)
 
 
 def line_parts(ni):
@@ -34,10 +34,10 @@
 
 
 def march_kernel(
-    counts, relay, now_hbm, old_hbm, speed_hbm, field, scaled, mean_ref, scale_ref,
-    work, face_out, face_in, rim_out, rim_in, own_stats, own_edge, in_stats, all_edge, relayed,
+    counts, relay, now_hbm, old_hbm, speed_hbm, field, scaled, own_edge, all_edge,
+    work, face_out, face_in, rim_out, rim_in, own_stats, in_stats, relayed,
     means, scales, load_rim, load_x, load_y, load_c,
-    side_send, side_recv, pass_send, pass_recv, row_send, row_recv, row_rim_recv,
+    side_send, side_recv, pass_send, row_send, row_recv, row_rim_recv,
     slab_send, slab_recv, slab_rim_recv, stat_send, edge_send, edge_recv,
 ):
     nj, ni, nk, lanes = now_hbm.shape
@@ -127,7 +127,7 @@
         sems = side_send.at[step % 2, which], side_recv.at[step % 2, which, j]
         if kind == "to":
             landing, target = relayed.at[step, j], over
-            sems = sems[0], pass_recv.at[step % 2, j]
+            sems = sems[0], side_recv.at[step % 2, DIAG, j]
         elif kind == "on":
             source, landing, target = relayed.at[step, j], buffer.at[j + 1, halos[OWN]], beside[OWN]
             sems = pass_send, sems[1]
@@ -163,12 +163,12 @@
         place = 2 if number == parts else ni - 1
         return place, place + 1
 
-    def slot(step, number):
-        return step % 2 * parts + number if number < parts else parts + number
+    def arrival(sems, strip_sem, step, number):
+        return sems.at[step % 2 * parts + number] if number < parts else load_c.at[strip_sem + number - parts]
 
     def rows(step, number, what):
         start, stop = segment(step, number)
-        lines, buffer, recv = pl.ds(start, stop - start), buffer_of(step), row_recv.at[slot(step, number)]
+        lines, buffer, recv = pl.ds(start, stop - start), buffer_of(step), arrival(row_recv, 0, step, number)
         if what == "taken":
             one, two = (buffer.at[pl.ds(0, n), lines] for n in (1, 2))
             send = row_send.at[step % 2, 0]
@@ -204,7 +204,7 @@
 
     def slabs(step, number, what):
         start, stop = segment(step, number)
-        lines, recv = pl.ds(start - 1, stop - start), slab_recv.at[slot(step, number)]
+        lines, recv = pl.ds(start - 1, stop - start), arrival(slab_recv, 2, step, number)
         if what == "taken":
             one, two = (face_in.at[step, pl.ds(0, n), lines] for n in (1, 2))
             taken("slabs", *(remote(some, some, slab_send.at[0], recv, "slabs", here["slabs"]) for some in (one, two)))
@@ -216,8 +216,10 @@
             )
             pl.when(there)(copy.start)
 
-    def slab_rim(step, which, j, what):
-        recv = slab_rim_recv.at[step % 2, which, j]
+    group = 2 if nj % 2 == 0 else 1
+
+    def slab_rim(step, which, pair, what):
+        recv, j = slab_rim_recv.at[step % 2, which, pair], pl.ds(group * pair, group)
         if what == "taken":
             one, two = (rim_in.at[step, pl.ds(0, n), which, j] for n in (1, 2))
             taken("slabs", *(remote(some, some, slab_send.at[0], recv, "slabs", here["slabs"]) for some in (one, two)))
@@ -248,8 +250,8 @@
             rim_out[0, 1, which, j] = work[j + 1, places[which], pl.ds(nk - 1, 1), :]
     for which in (OWN, DIAG):
         row_rim(0, which, (0, 1), "start")
-        for j in range(nj):
-            slab_rim(0, which, j, "start")
+        for pair in range(nj // group):
+            slab_rim(0, which, pair, "start")
 
     zeros_line = jnp.zeros((nk, lanes), jnp.float32)
     for buffer in (work, field):
@@ -353,7 +355,7 @@
                     own_edge[0, pl.ds(rim * nj + j, 1), :] = total
                     own_edge[1, pl.ds(rim * nj + j, 1), :] = square
 
-    every_j, begun = tuple(range(nj)), set()
+    every_j, begun, done = tuple(range(nj)), set(), {}
 
     def loaded(part):
         if ("load", part) not in begun:
@@ -396,7 +398,10 @@
 
     def edge(step, which, j):
         side(step - 1, which, j, "taken")
-        slab_rim(step - 1, which, j, "taken")
+        pair = (step, which, j // group)
+        done[pair] = done.get(pair, 0) + 1
+        if done[pair] == 1:
+            slab_rim(step - 1, which, j // group, "taken")
         shared = [to_high for to_high, place in ((0, 0), (1, nj - 1)) if place == j]
         row_rim(step - 1, which, [1 - to_high for to_high in shared], "taken")
         if step >= 2 and (step, which) not in begun:
@@ -411,7 +416,8 @@
                 side(0, DIAG, other, "start")
         if step < STEPS:
             side(step, which, j, "start")
-            slab_rim(step, which, j, "start")
+            if done[pair] == group:
+                slab_rim(step, which, j // group, "start")
             row_rim(step, which, shared, "start")
 
     levels = n_slabs.bit_length() - 1
@@ -489,18 +495,6 @@
     for part in outside_in:
         rescale(part)
 
-    def combine(own, others):
-        mean = own[0]
-        for other in others:
-            mean = mean + other[0]
-        mean = mean * (1.0 / whole)
-        square = None
-        for one in (own, *others):
-            gap = one[0] * (1.0 / nk) - mean
-            term = one[1] + nk * gap * gap
-            square = term if square is None else square + term
-        return mean, lax.rsqrt(square * (1.0 / whole) + EPS)
-
     for step in range(STEPS):
         if step == 2:
             for which in (OWN, DIAG):
@@ -508,13 +502,10 @@
             rows_sent(step)
     slabs_sent()
     if half:
-        pl.when(relays)(remote(relayed, relayed, pass_send, pass_recv.at[0, 0], "cols", beside[OWN]).wait_send)
+        pl.when(relays)(remote(relayed, relayed, pass_send, side_recv.at[0, DIAG, 0], "cols", beside[OWN]).wait_send)
     remote(own_stats, in_stats, stat_send, stat_recv[0].at[0], "slabs", partners[0]).wait_send()
     edges = remote(all_edge, all_edge, edge_send, edge_recv, "slabs", peers[0])
     edges.wait_recv()
-    mean, scale = combine(own_edge[...], [all_edge[gap - 1] for gap in gaps])
-    mean_ref[...] = mean
-    scale_ref[...] = scale
     edges.wait_send()
 
 
@@ -547,18 +538,30 @@
     return [entry for _, _, entry in sorted(timed, key=lambda spot: spot[:2])]
 
 
-def finish_kernel(field, scaled, mean_ref, scale_ref, scaled_hbm, field_hbm, rims, field_sem, scaled_sem):
+def finish_kernel(field, scaled, own_edge, all_edge, scaled_hbm, field_hbm, rims, field_sem, scaled_sem):
     nj, ni, nk, lanes = scaled_hbm.shape
     inner = pl.ds(1, ni - 2)
     for j in range(nj):
         pltpu.make_async_copy(field.at[j + 1, pl.ds(1, ni)], field_hbm.at[j], field_sem).start()
         pltpu.make_async_copy(scaled.at[j, inner], scaled_hbm.at[j, inner], scaled_sem).start()
+    pieces = [own_edge[...], *(all_edge[gap] for gap in range(all_edge.shape[0]))]
+    whole = float(nk * len(pieces))
+    means = pieces[0][0]
+    for piece in pieces[1:]:
+        means = means + piece[0]
+    means = means * (1.0 / whole)
+    square = None
+    for piece in pieces:
+        apart = piece[0] * (1.0 / nk) - means
+        term = piece[1] + nk * apart * apart
+        square = term if square is None else square + term
+    scales = lax.rsqrt(square * (1.0 / whole) + EPS)
     places = edge_places(lax.axis_index("cols"), ni)
     for which in (OWN, DIAG):
         for j in range(nj):
-            row = pl.ds(which * nj + j, 1)
-            mean = jnp.broadcast_to(mean_ref[row, :], (8, lanes))
-            scale = jnp.broadcast_to(scale_ref[row, :], (8, lanes))
+            row = which * nj + j
+            mean = jnp.broadcast_to(means[row:row + 1], (8, lanes))
+            scale = jnp.broadcast_to(scales[row:row + 1], (8, lanes))
             for g in range(nk // 8):
                 k = pl.ds(8 * g, 8)
                 rims[which, j, k, :] = (field[j + 1, places[which], k, :] - mean) * scale
@@ -580,14 +583,14 @@
     vmem = pl.BlockSpec(memory_space=pltpu.VMEM)
     cells = nj * ni * nk * lanes
     dma = pltpu.SemaphoreType.DMA
-    field, scaled, mean, scale = pl.pallas_call(
+    field, scaled, own_edge, all_edge = pl.pallas_call(
         functools.partial(march_kernel, counts, relay),
         name="march",
         out_shape=(
             pltpu.VMEM(padded, f32),
             pltpu.VMEM((nj, ni, nk, lanes), f32),
-            pltpu.VMEM((2 * nj, lanes), f32),
-            pltpu.VMEM((2 * nj, lanes), f32),
+            pltpu.VMEM((2, 2 * nj, lanes), f32),
+            pltpu.VMEM((n_slabs - 1, 2, 2 * nj, lanes), f32),
         ),
         in_specs=[hbm] * 3,
         out_specs=(vmem,) * 4,
@@ -598,26 +601,23 @@
             pltpu.VMEM((STEPS, 2, 2, nj, 1, lanes), f32),
             pltpu.VMEM((STEPS, 2, 2, nj, 1, lanes), f32),
             pltpu.VMEM((levels, 2, nj, ni, lanes), f32),
-            pltpu.VMEM((2, 2 * nj, lanes), f32),
             pltpu.VMEM((levels, 2, nj, ni, lanes), f32),
-            pltpu.VMEM((n_slabs - 1, 2, 2 * nj, lanes), f32),
             pltpu.VMEM((STEPS, max(nj // 2, 1), nk, lanes), f32),
             pltpu.VMEM((nj, ni, lanes), f32),
             pltpu.VMEM((nj, ni, lanes), f32),
             dma(()),
             dma((parts,)),
             dma((parts,)),
-            dma((parts,)),
+            dma((max(parts, 4),)),
             dma((2, 2)),
             dma((2, 2, nj)),
             dma(()),
-            dma((2, max(nj // 2, 1))),
             dma((2, 2)),
-            dma((2 * parts + 2,)),
+            dma((2 * parts,)),
             dma((2, 2, 2)),
             dma((2,)),
-            dma((2 * parts + 2,)),
-            dma((2, 2, nj)),
+            dma((2 * parts,)),
+            dma((2, 2, nj // (2 if nj % 2 == 0 else 1))),
             dma(()),
             dma(()),
             dma(()),
@@ -640,7 +640,7 @@
         ],
         compiler_params=pltpu.CompilerParams(vmem_limit_bytes=16 * 2**20),
         cost_estimate=pl.CostEstimate(flops=2 * cells, bytes_accessed=8 * cells, transcendentals=0),
-    )(field, scaled, mean, scale)
+    )(field, scaled, own_edge, all_edge)
 
 
 def crosses(mesh):

time: 43 us -> 41.5 us (0.965)
  Pallas kernels: 42.3 us -> 40.5 us
    pallas_call x1, Pallas kernels: 36.4 us -> 34.7 us  [shards(): pl.pallas_call(functools.partial(march_kernel, counts, relay), name='marc...]
where the time goes in v4:
time: 41.5 us; the launch traced here: 41.2 us
  Pallas kernels  40.5 us (98%)
  between operations  0.64 us (2%)
    pallas_call x1, Pallas kernels, shards(): pl.pallas_call(functools.partial(march_kernel, counts, relay), name='marc...  34.7 us
    pallas_call x1, Pallas kernels, shards(): pl.pallas_call(finish_kernel, name='finish', out_shape=(jax.ShapeDtypeStr...  5.86 us

profile of v4, /device:TPU:0, one launch (start us, length us, event | category | flops | bytes accessed | tf_op | source)
XLA Modules:
  0.0 41.2 jit_solution(14735718311004339072)
XLA Ops:
  0.6 34.7 %march.1 = (f32[6,34,128,128]{3,2,1,0:T(8,128)S(1)}, f32[4,32,128,128]{3,2,1,0:T(8,128)S(1)}, f32[2,8,128]{2,1,0:T(8,128)S(1)}, f32[3,2,8,128]{3,2,1,0:T(8,128)S(1)}) custom-call(f32[4,32,128,128]{3,2,1,0:T(8,128)} %now_hbm.1, f32[4,32,128,128]{3,2,1,0:T(8,128)} %old_hbm.1, f32[4,32,128,128]{3,2,1,0:T(8,128)} %speed_hbm.1), custom_call_target="tpu_custom_call" | custom-call | flops 69206016 | bytes 25165824 | tf_op jit(solution)/shard_map/march/pallas_call | solution.py:586
  35.3 5.9 %finish.1 = (f32[4,32,128,128]{3,2,1,0:T(8,128)}, f32[4,32,128,128]{3,2,1,0:T(8,128)}) custom-call(f32[6,34,128,128]{3,2,1,0:T(8,128)S(1)} %get-tuple-element.6.field, f32[4,32,128,128]{3,2,1,0:T(8,128)S(1)} %get-tuple-element.7.scaled, f32[2,8,128]{2,1,0:T(8,128)S(1)} %get-tuple-element.8.own_edge, f32[3,2,8,128]{3,2,1,0:T(8,128)S(1)} %get-tuple-element.9.all_edge), custom_call_target="tpu_custom_call" | custom-call | flops 4194304 | bytes 16777216 | tf_op jit(solution)/shard_map/finish/pallas_call | solution.py:630
